TPU v7x, 32 devices: a whole 2x2x4 slice. The times are simulated.
32 devices in a mesh: shard: 2 (over core), ctx: 4 (over y, x), tp: 4 (over z).
Axes of the slice: x: 2, y: 2, z: 4, core: 2. Of those that a mesh axis runs over, the one named last changes fastest.
Arguments:
- tokens: bfloat16 [2, 4096, 1024], P('shard', 'ctx'), may hold values from -6 to 6
- lengths: int32 [2], P('shard'), may hold values from 1024 to 4096, as said below
- routes: int32 [2, 4096, 1], P('shard', 'ctx'), may hold values from 0 to 7; in each aligned block of 1024 rows (0 to 1023, 1024 to 2047, ..., all dimensions but the last counted through in order) at most 384 rows name the same one
- priority: int32 [2, 4096], P('shard', 'ctx'), may hold values from 0 to 8191, as said below
- attn_gain: bfloat16 [1024], P(('shard', 'ctx')), may hold values from 0.5 to 1.5
- qkv_weight: bfloat16 [1024, 3, 1024], P(('shard', 'ctx'), None, 'tp'), may hold values from -0.1875 to 0.1875
- proj_weight: bfloat16 [1024, 1024], P('tp', ('shard', 'ctx')), may hold values from -2 to 2
- ffn_gain: bfloat16 [1024], P(('shard', 'ctx')), may hold values from 0.5 to 1.5
- mix_weight: bfloat16 [1024, 2], P(('shard', 'ctx')), may hold values from -0.1875 to 0.1875
- up_weight: bfloat16 [1024, 4096], P(('shard', 'ctx'), 'tp'), may hold values from -0.1875 to 0.1875
- down_weight: bfloat16 [4096, 1024], P('tp', ('shard', 'ctx')), may hold values from -0.09375 to 0.09375
- expert_up: bfloat16 [8, 1024, 4096], P(('shard', 'ctx'), None, 'tp'), may hold values from -0.1875 to 0.1875
- expert_down: bfloat16 [8, 4096, 1024], P(('shard', 'ctx'), 'tp'), may hold values from -0.09375 to 0.09375
- cotangent: bfloat16 [2, 4096, 1024], P('shard', 'ctx'), may hold values from -6 to 6
Outputs:
- layer_out: bfloat16 [2, 4096, 1024], P('shard', 'ctx')
- tokens_grad: bfloat16 [2, 4096, 1024], P('shard', 'ctx')
- attn_gain_grad: float32 [1024], P(('shard', 'ctx'))
- qkv_weight_grad: float32 [1024, 3, 1024], P(('shard', 'ctx'), None, 'tp')
- proj_weight_grad: float32 [1024, 1024], P('tp', ('shard', 'ctx'))
- ffn_gain_grad: float32 [1024], P(('shard', 'ctx'))
- mix_weight_grad: float32 [1024, 2], P(('shard', 'ctx'))
- up_weight_grad: float32 [1024, 4096], P(('shard', 'ctx'), 'tp')
- down_weight_grad: float32 [4096, 1024], P('tp', ('shard', 'ctx'))
- expert_up_grad: float32 [8, 1024, 4096], P(('shard', 'ctx'), None, 'tp')
- expert_down_grad: float32 [8, 4096, 1024], P(('shard', 'ctx'), 'tp')
Inputs may be any that keep to these rules, and one draw needn't show every extreme that they name: `lengths`: padding positions are those at or past a slot's length; some slot has exactly 4096 live positions. `routes`: in the rows of one device (one slot's 1024 positions on one index of ctx), at most 384 positions name the same expert, and exactly 384 do for some expert on some device. `priority`: each value 0 to 8191 occurs at exactly one position of all slots.
All inputs are finite; a program needn't handle non-finite values.
Results may differ from a plain program's by a relative error of at most 0.024.
Values may be sent and summed in bfloat16 or wider, within the bound.
A program may use at most 192 MiB of HBM per device.

v0:
```python
import jax
import jax.numpy as jnp
from jax import lax
from jax.sharding import PartitionSpec as P

HD = 64
CAP = 1152


empty_mark = 1 << 30
norm_eps = 1e-05
masked_score = -1e30


def gelu_tanh(values):
    return jax.nn.gelu(values, approximate=True)


def norm_forward(values, gain_vec):
    average = jnp.mean(values, axis=-1, keepdims=True)
    centred = values - average
    spread = jnp.mean(centred * centred, axis=-1, keepdims=True)
    inverse = lax.rsqrt(spread + norm_eps)
    unit_rows = centred * inverse
    return (unit_rows * gain_vec, unit_rows, inverse)


def norm_backward(upstream, gain_vec, unit_rows, inverse):
    shaped = upstream * gain_vec
    first_term = jnp.mean(shaped, axis=-1, keepdims=True)
    second_term = jnp.mean(shaped * unit_rows, axis=-1, keepdims=True)
    return (
        inverse * (shaped - first_term - unit_rows * second_term),
        jnp.sum(upstream * unit_rows, axis=0),
    )


def local(
    tokens,
    lengths,
    routes,
    priority,
    attn_gain,
    qkv_weight,
    proj_weight,
    ffn_gain,
    mix_weight,
    up_weight,
    down_weight,
    expert_up,
    expert_down,
    cotangent,
):
    seq_dev = tokens.shape[1]
    model_width = tokens.shape[2]
    full_len = seq_dev * lax.axis_size("ctx")
    positions = lax.axis_index("ctx") * seq_dev + jnp.arange(seq_dev, dtype=jnp.int32)
    live_mask = positions < lengths[0]
    live_rows = live_mask.astype(jnp.float32)[:, None]
    inputs = tokens[0].astype(jnp.float32)
    gain_one, qkv_full, proj_full, gain_two, mix_full, up_full, down_full = (
        lax.all_gather(attn_gain, ("shard", "ctx"), axis=0, tiled=True),
        lax.all_gather(qkv_weight, ("shard", "ctx"), axis=0, tiled=True),
        lax.all_gather(proj_weight, ("shard", "ctx"), axis=1, tiled=True),
        lax.all_gather(ffn_gain, ("shard", "ctx"), axis=0, tiled=True),
        lax.all_gather(mix_weight, ("shard", "ctx"), axis=0, tiled=True),
        lax.all_gather(up_weight, ("shard", "ctx"), axis=0, tiled=True),
        lax.all_gather(down_weight, ("shard", "ctx"), axis=1, tiled=True),
    )
    gain_one = gain_one.astype(jnp.float32)
    gain_two = gain_two.astype(jnp.float32)
    local_heads = qkv_full.shape[2] // HD
    score_scale = HD ** (-0.5)
    normed, unit_one, inverse_one = norm_forward(inputs, gain_one)
    normed_low = normed.astype(jnp.bfloat16)
    projected = jnp.einsum(
        "td,dcf->tcf", normed_low, qkv_full, preferred_element_type=jnp.float32
    ).astype(jnp.bfloat16)
    queries = projected[:, 0].reshape(seq_dev, local_heads, HD)
    keys_all, values_all = (
        lax.all_gather(projected[:, 1], "ctx", axis=0, tiled=True),
        lax.all_gather(projected[:, 2], "ctx", axis=0, tiled=True),
    )
    key_block = min(full_len, 1024)
    block_count = full_len // key_block
    key_blocks = keys_all.reshape(block_count, key_block, local_heads, HD)
    value_blocks = values_all.reshape(block_count, key_block, local_heads, HD)
    key_places = jnp.arange(full_len, dtype=jnp.int32).reshape(block_count, key_block)

    def allowed(places):
        return ((places[None, :] <= positions[:, None]) & (places[None, :] < lengths[0]))[None]

    def forward_step(state_now, pieces):
        running_max, running_sum, weighted = state_now
        key_rows, value_rows, places = pieces
        visible = allowed(places)
        scores = (
            jnp.einsum("qhd,khd->hqk", queries, key_rows, preferred_element_type=jnp.float32)
            * score_scale
        )
        scores = jnp.where(visible, scores, masked_score)
        new_max = jnp.maximum(running_max, jnp.max(scores, axis=-1))
        weights = jnp.where(visible, jnp.exp(scores - new_max[..., None]), 0.0)
        shrink = jnp.exp(running_max - new_max)
        running_sum = running_sum * shrink + jnp.sum(weights, axis=-1)
        weighted = weighted * shrink[..., None] + jnp.einsum(
            "hqk,khd->hqd",
            weights.astype(jnp.bfloat16),
            value_rows,
            preferred_element_type=jnp.float32,
        )
        return ((new_max, running_sum, weighted), None)

    start_state = (
        jnp.full((local_heads, seq_dev), masked_score, jnp.float32),
        jnp.zeros((local_heads, seq_dev), jnp.float32),
        jnp.zeros((local_heads, seq_dev, HD), jnp.float32),
    )
    (running_max, running_sum, weighted), _ = lax.scan(
        forward_step, start_state, (key_blocks, value_blocks, key_places)
    )
    log_total = running_max + jnp.log(running_sum)
    heads_out = weighted / running_sum[..., None]
    attended_low = jnp.transpose(heads_out, (1, 0, 2)).reshape(seq_dev, -1).astype(jnp.bfloat16)
    branch_part = jnp.dot(attended_low, proj_full, preferred_element_type=jnp.float32)
    branch = lax.psum(branch_part.astype(jnp.bfloat16), "tp").astype(jnp.float32)
    middle = inputs + branch
    normed2, unit_two, inverse_two = norm_forward(middle, gain_two)
    normed2_low = normed2.astype(jnp.bfloat16)
    mixing = jax.nn.softmax(
        jnp.dot(normed2_low, mix_full, preferred_element_type=jnp.float32), axis=-1
    )
    upper_pre = jnp.dot(normed2_low, up_full, preferred_element_type=jnp.float32)
    hidden_low = gelu_tanh(upper_pre).astype(jnp.bfloat16)
    dense_part = jnp.dot(hidden_low, down_full, preferred_element_type=jnp.float32)
    experts_total = lax.axis_size(("shard", "ctx"))
    slot_cap = max(4, 3 * seq_dev // experts_total)
    chosen = routes[0, :, 0]
    onehot = (chosen[:, None] == jnp.arange(experts_total, dtype=jnp.int32)[None, :]).astype(
        jnp.int32
    )
    slot_pos = jnp.sum(jnp.cumsum(onehot, axis=0) * onehot, axis=1) - 1
    target = jnp.where(live_mask, chosen * slot_cap + slot_pos, experts_total * slot_cap)

    def pack_rows(token_rows):
        buffer = jnp.zeros((experts_total * slot_cap, model_width), token_rows.dtype)
        return (
            buffer.at[target]
            .set(token_rows, mode="drop")
            .reshape(experts_total, slot_cap, model_width)
        )

    send_order = (
        jnp.full((experts_total * slot_cap,), empty_mark, jnp.int32)
        .at[target]
        .set(priority[0], mode="drop")
    )
    recv_rows, recv_order = (
        lax.all_to_all(
            pack_rows(normed2_low), ("shard", "ctx"), split_axis=0, concat_axis=0, tiled=True
        ),
        lax.all_to_all(
            send_order.reshape(experts_total, slot_cap),
            ("shard", "ctx"),
            split_axis=0,
            concat_axis=0,
            tiled=True,
        ),
    )
    flat_order = recv_order.reshape(-1)
    ranking = jnp.argsort(flat_order)[:CAP]
    taken_mask = (flat_order[ranking] < empty_mark).astype(jnp.float32)[:, None]
    expert_in = recv_rows.reshape(-1, model_width)[ranking]
    own_up = expert_up[0]
    own_down = expert_down[0]
    expert_pre = jnp.dot(expert_in, own_up, preferred_element_type=jnp.float32)
    expert_hidden = gelu_tanh(expert_pre).astype(jnp.bfloat16)
    expert_part = jnp.dot(expert_hidden, own_down, preferred_element_type=jnp.float32) * taken_mask

    def unfold_rows(slot_rows):
        buffer = jnp.zeros((experts_total * slot_cap, model_width), jnp.float32)
        return buffer.at[ranking].set(slot_rows).reshape(experts_total, slot_cap, model_width)

    full_index = jnp.where(live_mask, chosen * slot_cap + slot_pos, 0)
    returned_rows = lax.all_to_all(
        unfold_rows(expert_part).astype(jnp.bfloat16),
        ("shard", "ctx"),
        split_axis=0,
        concat_axis=0,
        tiled=True,
    ).astype(jnp.float32)
    expert_tok = returned_rows.reshape(-1, model_width)[full_index] * live_rows
    mixed_part = mixing[:, 0:1] * dense_part + mixing[:, 1:2] * expert_tok
    mixed = lax.psum(mixed_part.astype(jnp.bfloat16), "tp").astype(jnp.float32)
    layer_out = ((middle + mixed) * live_rows).astype(jnp.bfloat16)[None]
    out_grad = cotangent[0].astype(jnp.float32) * live_rows
    dense_grad = (mixing[:, 0:1] * out_grad).astype(jnp.bfloat16)
    expert_grad = (mixing[:, 1:2] * out_grad).astype(jnp.bfloat16)
    dots_part = jnp.stack(
        [jnp.sum(out_grad * dense_part, axis=-1), jnp.sum(out_grad * expert_tok, axis=-1)], axis=-1
    )
    down_grad = jnp.einsum("tf,td->fd", hidden_low, dense_grad, preferred_element_type=jnp.float32)
    hidden_grad = jnp.einsum("td,fd->tf", dense_grad, down_full, preferred_element_type=jnp.float32)
    _, gelu_pull = jax.vjp(gelu_tanh, upper_pre)
    upper_grad = gelu_pull(hidden_grad)[0].astype(jnp.bfloat16)
    up_grad = jnp.einsum("td,tf->df", normed2_low, upper_grad, preferred_element_type=jnp.float32)
    normed2_part = jnp.einsum("tf,df->td", upper_grad, up_full, preferred_element_type=jnp.float32)
    recv_grad = lax.all_to_all(
        pack_rows(expert_grad), ("shard", "ctx"), split_axis=0, concat_axis=0, tiled=True
    )
    grad_in = recv_grad.reshape(-1, model_width)[ranking]
    own_down_grad = jnp.einsum(
        "cf,cd->fd", expert_hidden, grad_in, preferred_element_type=jnp.float32
    )
    ehidden_grad = jnp.einsum("cd,fd->cf", grad_in, own_down, preferred_element_type=jnp.float32)
    _, expert_pull = jax.vjp(gelu_tanh, expert_pre)
    epre_grad = expert_pull(ehidden_grad)[0].astype(jnp.bfloat16)
    own_up_grad = jnp.einsum("cd,cf->df", expert_in, epre_grad, preferred_element_type=jnp.float32)
    expert_in_grad = jnp.einsum("cf,df->cd", epre_grad, own_up, preferred_element_type=jnp.float32)
    sent_back = lax.all_to_all(
        unfold_rows(expert_in_grad).astype(jnp.bfloat16),
        ("shard", "ctx"),
        split_axis=0,
        concat_axis=0,
        tiled=True,
    ).astype(jnp.float32)
    expert_tok_grad = sent_back.reshape(-1, model_width)[full_index] * live_rows
    normed2_grad, branch_dots = (
        lax.psum((normed2_part + expert_tok_grad).astype(jnp.bfloat16), "tp").astype(jnp.float32),
        lax.psum(dots_part.astype(jnp.bfloat16), "tp").astype(jnp.float32),
    )
    logit_grad = mixing * (branch_dots - jnp.sum(mixing * branch_dots, axis=-1, keepdims=True))
    mix_grad = jnp.dot(
        normed2_low.astype(jnp.float32).T, logit_grad, precision=lax.Precision.HIGHEST
    )
    normed2_grad = normed2_grad + jnp.dot(
        logit_grad, mix_full.astype(jnp.float32).T, precision=lax.Precision.HIGHEST
    )
    middle_norm_grad, gain_two_grad = norm_backward(normed2_grad, gain_two, unit_two, inverse_two)
    middle_grad = out_grad + middle_norm_grad
    branch_grad = middle_grad.astype(jnp.bfloat16)
    proj_grad = jnp.einsum(
        "tf,td->fd", attended_low, branch_grad, preferred_element_type=jnp.float32
    )
    attended_grad = jnp.einsum(
        "td,fd->tf", branch_grad, proj_full, preferred_element_type=jnp.float32
    ).astype(jnp.bfloat16)
    grad_heads = attended_grad.reshape(seq_dev, local_heads, HD)
    row_delta = jnp.sum(
        jnp.transpose(grad_heads, (1, 0, 2)).astype(jnp.float32) * heads_out, axis=-1
    )

    def backward_step(query_grad, pieces):
        key_rows, value_rows, places = pieces
        visible = allowed(places)
        scores = (
            jnp.einsum("qhd,khd->hqk", queries, key_rows, preferred_element_type=jnp.float32)
            * score_scale
        )
        probs = jnp.where(visible, jnp.exp(scores - log_total[..., None]), 0.0)
        prob_grad = jnp.einsum(
            "qhd,khd->hqk", grad_heads, value_rows, preferred_element_type=jnp.float32
        )
        score_grad = (probs * (prob_grad - row_delta[..., None])).astype(jnp.bfloat16)
        query_grad = query_grad + jnp.einsum(
            "hqk,khd->qhd", score_grad, key_rows, preferred_element_type=jnp.float32
        )
        key_grad = jnp.einsum(
            "hqk,qhd->khd", score_grad, queries, preferred_element_type=jnp.float32
        )
        value_grad = jnp.einsum(
            "hqk,qhd->khd",
            probs.astype(jnp.bfloat16),
            grad_heads,
            preferred_element_type=jnp.float32,
        )
        return (query_grad, (key_grad, value_grad))

    query_grad, (key_grad_blocks, value_grad_blocks) = lax.scan(
        backward_step,
        jnp.zeros((seq_dev, local_heads, HD), jnp.float32),
        (key_blocks, value_blocks, key_places),
    )
    key_grad_all = key_grad_blocks.reshape(full_len, -1) * score_scale
    value_grad_all = value_grad_blocks.reshape(full_len, -1)
    key_grad_own, value_grad_own = (
        lax.psum_scatter(
            key_grad_all.astype(jnp.bfloat16), "ctx", scatter_dimension=0, tiled=True
        ).astype(jnp.float32),
        lax.psum_scatter(
            value_grad_all.astype(jnp.bfloat16), "ctx", scatter_dimension=0, tiled=True
        ).astype(jnp.float32),
    )
    qkv_grad = jnp.stack(
        [(query_grad * score_scale).reshape(seq_dev, -1), key_grad_own, value_grad_own], axis=1
    ).astype(jnp.bfloat16)
    qkv_grad_full = jnp.einsum(
        "td,tcf->dcf", normed_low, qkv_grad, preferred_element_type=jnp.float32
    )
    normed_part = jnp.einsum("tcf,dcf->td", qkv_grad, qkv_full, preferred_element_type=jnp.float32)
    normed_grad = lax.psum(normed_part.astype(jnp.bfloat16), "tp").astype(jnp.float32)
    input_norm_grad, gain_one_grad = norm_backward(normed_grad, gain_one, unit_one, inverse_one)
    tokens_grad = (middle_grad + input_norm_grad).astype(jnp.bfloat16)[None]
    shares = (
        lax.psum_scatter(gain_one_grad, ("shard", "ctx"), scatter_dimension=0, tiled=True),
        lax.psum_scatter(qkv_grad_full, ("shard", "ctx"), scatter_dimension=0, tiled=True),
        lax.psum_scatter(proj_grad, ("shard", "ctx"), scatter_dimension=1, tiled=True),
        lax.psum_scatter(gain_two_grad, ("shard", "ctx"), scatter_dimension=0, tiled=True),
        lax.psum_scatter(mix_grad, ("shard", "ctx"), scatter_dimension=0, tiled=True),
        lax.psum_scatter(up_grad, ("shard", "ctx"), scatter_dimension=0, tiled=True),
        lax.psum_scatter(down_grad, ("shard", "ctx"), scatter_dimension=1, tiled=True),
    )
    return (
        layer_out,
        tokens_grad,
        shares[0],
        shares[1],
        shares[2],
        shares[3],
        shares[4],
        shares[5],
        shares[6],
        own_up_grad[None],
        own_down_grad[None],
    )


def solution(mesh):
    placed = (
        P("shard", "ctx", None),
        P("shard"),
        P("shard", "ctx", None),
        P("shard", "ctx"),
        P(("shard", "ctx")),
        P(("shard", "ctx"), None, "tp"),
        P("tp", ("shard", "ctx")),
        P(("shard", "ctx")),
        P(("shard", "ctx"), None),
        P(("shard", "ctx"), "tp"),
        P("tp", ("shard", "ctx")),
        P(("shard", "ctx"), None, "tp"),
        P(("shard", "ctx"), "tp", None),
        P("shard", "ctx", None),
    )
    return jax.shard_map(
        local,
        mesh=mesh,
        in_specs=placed,
        out_specs=(
            P("shard", "ctx", None),
            P("shard", "ctx", None),
            P(("shard", "ctx")),
            P(("shard", "ctx"), None, "tp"),
            P("tp", ("shard", "ctx")),
            P(("shard", "ctx")),
            P(("shard", "ctx"), None),
            P(("shard", "ctx"), "tp"),
            P("tp", ("shard", "ctx")),
            P(("shard", "ctx"), None, "tp"),
            P(("shard", "ctx"), "tp", None),
        ),
        check_vma=False,
    )
```

profile of v0, /device:TPU:0, one launch (start us, length us, event | category | flops | bytes accessed | tf_op | source)
XLA Modules:
  0.0 1538.6 jit_solution(16928028134594946048)
XLA Ops:
  9.2 15.0 all-gather.2
  28.5 10.5 all-gather.10.cloned.1.call-done
  45.0 24.4 %all_gather.31 = bf16[256,1024]{1,0:T(8,128)(2,1)S(1)} all-gather(bf16[256,128]{1,0:T(8,128)(2,1)S(1)} %copy-done.32), channel_id=1, replica_groups=mesh['shard'=2,'ctx'=4,'tp'=4] {'shard','ctx'}, dimensions={1}, use_global_device_ids=true | all-gather | bytes 589824 | tf_op jit(solution)/shard_map/all_gather | solution.py:64
  69.4 13.8 all-gather.18.cloned.1.call-done
  91.3 29.6 %all-gather.16.cloned.1.call-done = bf16[4096,1,256]{0,2,1:T(8,128)(2,1)} async-done(((bf16[1024,1,256]{0,2,1:T(8,128)(2,1)}), bf16[4096,1,256]{0,2,1:T(8,128)(2,1)}) %all-gather.16.cloned.1.call-update) | async-done | bytes 2097168 | tf_op jit(solution)/shard_map/all_gather | solution.py:81
  128.9 67.9 %while.30 = (s32[]{:T(128)}, f32[4,1024]{1,0:T(4,128)S(1)}, f32[4,1024]{1,0:T(4,128)S(1)}, f32[4,1024,64]{1,2,0:T(8,128)}, s32[4,1024]{1,0:T(4,128)S(1)}, /*inde...) while((s32[]{:T(128)}, f32[4,1024]{1,0:T(4,128)S(1)}, ...), condition=%wide.region_5.6_spmd.clone, body=%wide.region_2.5_spmd.clone.sunk | while | flops 1131173888 | bytes 66869456 | solution.py:119
  213.3 14.5 all-gather.3
  227.8 59.8 %all-reduce.8.cloned.1.call-done = bf16[1024,1024]{1,0:T(8,128)(2,1)} async-done(((bf16[1024,1024]{1,0:T(8,128)(2,1)}), bf16[1024,1024]{1,0:T(8,128)(2,1)}) %all-reduce.8.cloned.1.call-update) | async-done | bytes 2097168 | tf_op jit(solution)/shard_map/psum | solution.py:126
  294.8 9.8 scatter_custom_fusion.1
  322.2 66.5 %all-to-all-done.1 = bf16[8,384,1024]{2,1,0:T(8,128)(2,1)} async-done(((bf16[8,384,1024]{2,1,0:T(8,128)(2,1)}), bf16[8,384,1024]{2,1,0:T(8,128)(2,1)}, u32[]{:S(2)}, u32[]{:S(2)}) %all-to-all-start.1) | async-done | bytes 6291488 | tf_op jit(solution)/shard_map/all_to_all | solution.py:159
  388.8 10.2 gather_fusion
  410.7 14.5 scatter_custom_fusion.2
  438.9 86.6 %all_gather.33 = bf16[1024,2]{0,1:T(2,128)(2,1)S(1)} all-gather(bf16[128,2]{0,1:T(2,128)(2,1)S(1)} %copy-done.54), channel_id=1, replica_groups=mesh['shard'=2,'ctx'=4,'tp'=4] {'shard','ctx'}, dimensions={0}, use_global_device_ids=true | all-gather | bytes 4608 | tf_op jit(solution)/shard_map/all_gather | solution.py:66
  543.2 10.9 gather_fusion.2
  554.1 9.6 fusion.91
  563.7 10.0 psum.38
  573.8 10.1 scatter_custom_fusion.3
  583.9 76.7 %all_to_all.29 = bf16[8,384,1024]{2,1,0:T(8,128)(2,1)} all-to-all(bf16[8,384,1024]{2,1,0:T(8,128)(2,1)} %bitcast.322), channel_id=1, replica_groups=mesh['shard'=2,'ctx'=4,'tp'=4] {'shard','ctx'}, dimensions={0} | all-to-all | bytes 12582912 | tf_op jit(solution)/shard_map/all_to_all | solution.py:208
  660.6 10.2 gather_fusion.3
  684.5 14.3 scatter_custom_fusion.4
  720.6 62.3 %all-to-all-done.4 = bf16[8,384,1024]{2,1,0:T(8,128)(2,1)} async-done(((bf16[8,384,1024]{2,1,0:T(8,128)(2,1)}), bf16[8,384,1024]{2,1,0:T(8,128)(2,1)}, u32[]{:S(2)}, u32[]{:S(2)}) %all-to-all-start.4) | async-done | bytes 6291488 | tf_op jit(solution)/shard_map/all_to_all | solution.py:220
  791.8 11.0 gather_fusion.4
  810.2 83.1 %all-reduce.10.cloned.1.call-done = bf16[1024,1024]{1,0:T(8,128)(2,1)} async-done(((bf16[1024,1024]{1,0:T(8,128)(2,1)}), bf16[1024,1024]{1,0:T(8,128)(2,1)}) %all-reduce.10.cloned.1.call-update) | async-done | bytes 2097168 | tf_op jit(solution)/shard_map/psum | solution.py:229
  907.0 144.0 %while.31 = (s32[]{:T(128)}, f32[1024,4,64]{0,2,1:T(8,128)S(1)}, f32[4,1024,4,64]{1,3,2,0:T(8,128)}, bf16[4,1024,4,64]{1,3,2,0:T(8,128)(2,1)}, bf16[4,1024,4,64]...) while((s32[]{:T(128)}, f32[1024,4,64]{0,2,1:T(8,128)S(1)}, ...), condition=%wide.region_30.31_spmd.clone, body=%wide.region_29.30_spmd.clone.sunk | while | flops 2728921088 | bytes 86579392 | solution.py:279
  1085.2 14.1 reduce-scatter.12.cloned.1.call-done
  1099.3 38.2 %reduce-scatter.10.cloned.1.call-done = bf16[1024,256]{1,0:T(8,128)(2,1)} async-done(((bf16[4096,256]{1,0:T(8,128)(2,1)}), bf16[1024,256]{1,0:T(8,128)(2,1)}) %reduce-scatter.10.cloned.1.call-update) | async-done | bytes 524304 | tf_op jit(solution)/shard_map/reduce_scatter | solution.py:287
  1189.0 144.2 %all-reduce.12.cloned.1.call-done = (bf16[1024,1024]{1,0:T(8,128)(2,1)}, bf16[1024,1024]{1,0:T(8,128)(2,1)}) async-done(((bf16[1024,1024]{1,0:T(8,128)(2,1)}, bf16[1024,1024]{1,0:T(8,128)(2,1)}), (bf16[1024,1024]{1,0:T(8,128)(2,1)}, bf16[1024,1024]{1,0:T(8,128)(2,1)})) %all-reduce.12.cloned.1.call-update) | async-done | bytes 4194320 | tf_op jit(solution)/shard_map/psum | solution.py:194
  1336.7 14.7 all-reduce.2
  1359.8 27.3 %reduce-scatter.20.cloned.1.call-done = f32[1024,128]{1,0:T(8,128)} async-done(((f32[1024,1024]{1,0:T(8,128)}), f32[1024,128]{1,0:T(8,128)}) %reduce-scatter.20.cloned.1.call-update) | async-done | bytes 524304 | tf_op jit(solution)/shard_map/reduce_scatter | solution.py:311
  1387.0 55.1 %reduce-scatter.18.cloned.1.call-done = f32[128,1024]{1,0:T(8,128)} async-done(((f32[1024,1024]{1,0:T(8,128)}), f32[128,1024]{1,0:T(8,128)}) %reduce-scatter.18.cloned.1.call-update) | async-done | bytes 524304 | tf_op jit(solution)/shard_map/reduce_scatter | solution.py:310
  1442.2 39.6 %reduce-scatter.16.cloned.1.call-done = f32[256,128]{1,0:T(8,128)} async-done(((f32[256,1024]{1,0:T(8,128)}), f32[256,128]{1,0:T(8,128)}) %reduce-scatter.16.cloned.1.call-update) | async-done | bytes 131088 | tf_op jit(solution)/shard_map/reduce_scatter | solution.py:307
  1481.8 49.9 %reduce-scatter.14.cloned.1.call-done = f32[128,3,256]{2,0,1:T(8,128)} async-done(((f32[1024,3,256]{2,0,1:T(8,128)}), f32[128,3,256]{2,0,1:T(8,128)}) %reduce-scatter.14.cloned.1.call-update) | async-done | bytes 393232 | tf_op jit(solution)/shard_map/reduce_scatter | solution.py:306
  (333 shorter events, 485.1 us)
Async XLA Ops:
  7.2 398.9 %copy-start = (bf16[1,1024,1024]{2,1,0:T(8,128)(2,1)S(1)}, bf16[1,1024,1024]{2,1,0:T(8,128)(2,1)}, u32[]{:S(2)}) copy-start(bf16[1,1024,1024]{2,1,0:T(8,128)(2,1)} %param.30) | copy-start | bytes 6291460
  7.2 31.8 %all-gather.10.cloned.1.call-start = ((), (), s32[]{:S(2)}) async-start(), calls=%async_computation.12 | async-start | bytes 1769472 | tf_op jit(solution)/shard_map/all_gather | solution.py:63
  9.1 74.1 %all-gather.18.cloned.1.call-start = ((), (), s32[]{:S(2)}) async-start(), calls=%async_computation.24 | async-start | bytes 2621440 | tf_op jit(solution)/shard_map/all_gather | solution.py:82
  44.2 76.8 %all-gather.16.cloned.1.call-start = ((), (), s32[]{:S(2)}) async-start(), calls=%async_computation.23 | async-start | bytes 2621440 | tf_op jit(solution)/shard_map/all_gather | solution.py:81
  44.9 242.7 %all-reduce.8.cloned.1.call-start = ((), (), s32[]{:S(2)}) async-start(), calls=%async_computation.13 | async-start | bytes 4194304 | tf_op jit(solution)/shard_map/psum | solution.py:126
  69.4 129.0 %copy-start.14 = (bf16[256,1024]{1,0:T(8,128)(2,1)}, bf16[256,1024]{1,0:T(8,128)(2,1)S(1)}, u32[]{:S(2)}) copy-start(bf16[256,1024]{1,0:T(8,128)(2,1)S(1)} %all_gather.31) | copy-start | bytes 1572868
  196.9 93.8 %copy-start.23 = (f32[4,1024]{1,0:T(4,128)}, f32[4,1024]{1,0:T(4,128)S(1)}, u32[]{:S(2)}) copy-start(f32[4,1024]{1,0:T(4,128)S(1)} %get-tuple-element.138) | copy-start | bytes 49156
  196.9 93.8 %copy-start.25 = (f32[4,1024]{1,0:T(4,128)}, f32[4,1024]{1,0:T(4,128)S(1)}, u32[]{:S(2)}) copy-start(f32[4,1024]{1,0:T(4,128)S(1)} %get-tuple-element.136) | copy-start | bytes 49156
  196.9 93.8 %copy-start.27 = (s32[4,1024]{1,0:T(4,128)}, s32[4,1024]{1,0:T(4,128)S(1)}, u32[]{:S(2)}) copy-start(s32[4,1024]{1,0:T(4,128)S(1)} %get-tuple-element.679) | copy-start | bytes 49156
  209.9 94.7 %all-to-all-start = ((s32[8,1,384]{2,1,0:T(1,128)}), s32[8,1,384]{2,1,0:T(1,128)S(1)}, u32[]{:S(2)}, u32[]{:S(2)}) async-start(s32[8,1,384]{2,1,0:T(1,128)} %bitcast.19), calls=%async_computation | async-start | bytes 24576 | tf_op jit(solution)/shard_map/all_to_all | solution.py:162
  304.6 84.1 %all-to-all-start.1 = ((bf16[8,384,1024]{2,1,0:T(8,128)(2,1)}), bf16[8,384,1024]{2,1,0:T(8,128)(2,1)}, u32[]{:S(2)}, u32[]{:S(2)}) async-start(bf16[8,384,1024]{2,1,0:T(8,128)(2,1)} %bitcast.321), calls=%async_computation.1 | async-start | bytes 12582912 | tf_op jit(solution)/shard_map/all_to_all | solution.py:159
  309.4 218.4 %all-gather.12.cloned.1.call-start = ((), (), s32[]{:S(2)}) async-start(), calls=%async_computation.14 | async-start | bytes 2359296 | tf_op jit(solution)/shard_map/all_gather | solution.py:67
  433.3 101.0 %all-to-all-start.2 = ((bf16[8,384,1024]{2,1,0:T(8,128)(2,1)}), bf16[8,384,1024]{2,1,0:T(8,128)(2,1)}, u32[]{:S(2)}, u32[]{:S(2)}) async-start(bf16[8,384,1024]{2,1,0:T(8,128)(2,1)} %bitcast.323), calls=%async_computation.2 | async-start | bytes 12582912 | tf_op jit(solution)/shard_map/all_to_all | solution.py:185
  438.3 115.8 %all-gather.14.cloned.1.call-start = ((), (), s32[]{:S(2)}) async-start(), calls=%async_computation.15 | async-start | bytes 2359296 | tf_op jit(solution)/shard_map/all_gather | solution.py:68
  525.4 374.7 %copy-start.30 = (f32[1024]{0:T(1024)}, f32[1024]{0:T(1024)S(1)}, u32[]{:S(2)}) copy-start(f32[1024]{0:T(1024)S(1)} %fusion.129) | copy-start | bytes 12292
  573.7 319.6 %copy-start.37 = (bf16[1024,2]{0,1:T(2,128)(2,1)}, bf16[1024,2]{0,1:T(2,128)(2,1)S(1)}, u32[]{:S(2)}) copy-start(bf16[1024,2]{0,1:T(2,128)(2,1)S(1)} %psum.38) | copy-start | bytes 12292
  573.8 319.5 %copy-start.28 = (f32[1024,2]{0,1:T(2,128)}, f32[1024,2]{0,1:T(2,128)S(1)}, u32[]{:S(2)}) copy-start(f32[1024,2]{0,1:T(2,128)S(1)} %get-tuple-element.357) | copy-start | bytes 24580
  573.8 319.5 %copy-start.50 = (f32[1024]{0:T(1024)}, f32[1024]{0:T(1024)S(1)}, u32[]{:S(2)}) copy-start(f32[1024]{0:T(1024)S(1)} %get-tuple-element.356) | copy-start | bytes 12292
  573.8 326.3 %copy-start.48 = (f32[1024,1]{0,1:T(1,128)}, f32[1024,1]{0,1:T(1,128)S(1)}, u32[]{:S(2)}) copy-start(f32[1024,1]{0,1:T(1,128)S(1)} %get-tuple-element.365) | copy-start | bytes 12292
  707.0 75.9 %all-to-all-start.4 = ((bf16[8,384,1024]{2,1,0:T(8,128)(2,1)}), bf16[8,384,1024]{2,1,0:T(8,128)(2,1)}, u32[]{:S(2)}, u32[]{:S(2)}) async-start(bf16[8,384,1024]{2,1,0:T(8,128)(2,1)} %bitcast.324), calls=%async_computation.4 | async-start | bytes 12582912 | tf_op jit(solution)/shard_map/all_to_all | solution.py:220
  711.9 181.4 %all-reduce.10.cloned.1.call-start = ((), (), s32[]{:S(2)}) async-start(), calls=%async_computation.16 | async-start | bytes 4194304 | tf_op jit(solution)/shard_map/psum | solution.py:229
  802.8 90.6 %copy-start.45 = (f32[8,1,128]{2,1,0:T(1,128)S(1)}, f32[8,1,128]{2,1,0:T(1,128)}, u32[]{:S(2)}) copy-start(f32[8,1,128]{2,1,0:T(1,128)} %copy-done.44) | copy-start | bytes 12292
  810.1 289.2 %reduce-scatter.12.cloned.1.call-start = ((), (), s32[]{:S(2)}) async-start(), calls=%async_computation.18 | async-start | bytes 2621440 | tf_op jit(solution)/shard_map/reduce_scatter | solution.py:290
  1064.9 72.6 %reduce-scatter.10.cloned.1.call-start = ((), (), s32[]{:S(2)}) async-start(), calls=%async_computation.17 | async-start | bytes 2621440 | tf_op jit(solution)/shard_map/reduce_scatter | solution.py:287
  1079.8 95.3 %reduce-scatter.22.cloned.1.call-start = ((), (), s32[]{:S(2)}) async-start(), calls=%async_computation.25 | async-start | bytes 589824
  1083.0 250.2 %all-reduce.12.cloned.1.call-start = ((), (), s32[]{:S(2)}) async-start(), calls=%async_computation.26 | async-start | bytes 8388608 | tf_op jit(solution)/shard_map/psum | solution.py:194
  1142.4 244.7 %reduce-scatter.20.cloned.1.call-start = ((), (), s32[]{:S(2)}) async-start(), calls=%async_computation.22 | async-start | bytes 4718592 | tf_op jit(solution)/shard_map/reduce_scatter | solution.py:311
  1151.1 291.1 %reduce-scatter.18.cloned.1.call-start = ((), (), s32[]{:S(2)}) async-start(), calls=%async_computation.21 | async-start | bytes 4718592 | tf_op jit(solution)/shard_map/reduce_scatter | solution.py:310
  1157.2 324.6 %reduce-scatter.16.cloned.1.call-start = ((), (), s32[]{:S(2)}) async-start(), calls=%async_computation.20 | async-start | bytes 1179648 | tf_op jit(solution)/shard_map/reduce_scatter | solution.py:307
  1162.1 369.6 %reduce-scatter.14.cloned.1.call-start = ((), (), s32[]{:S(2)}) async-start(), calls=%async_computation.19 | async-start | bytes 3538944 | tf_op jit(solution)/shard_map/reduce_scatter | solution.py:306
  1189.0 147.7 %copy-start.52 = (f32[1024]{0:T(1024)S(1)}, f32[1024]{0:T(1024)}, u32[]{:S(2)}) copy-start(f32[1024]{0:T(1024)} %get-tuple-element.292) | copy-start | bytes 12292
  1352.6 179.1 %copy-start.1 = (bf16[1,1024,1024]{2,1,0:T(8,128)(2,1)S(1)}, bf16[1,1024,1024]{2,1,0:T(8,128)(2,1)}, u32[]{:S(2)}) copy-start(bf16[1,1024,1024]{2,1,0:T(8,128)(2,1)} %param.30) | copy-start | bytes 6291460
  (54 other events, 612.7 us)
Sparse Core Ops, SparseCore 0:
  10.5 28.4 all-gather.9
  44.3 38.9 all-gather.17
  85.7 35.1 all-gather.15
  201.4 86.1 all-reduce.7
  311.7 59.7 all-gather.11
  440.7 60.1 all-gather.13
  810.2 83.0 all-reduce.9
  1065.1 34.2 reduce-scatter.11
  1102.3 35.1 reduce-scatter.9
  1141.0 34.1 reduce-scatter.21
  1178.2 155.0 all-reduce.11
  1337.0 50.0 reduce-scatter.19
  1391.0 51.1 reduce-scatter.17
  1445.8 35.9 reduce-scatter.15
  1485.6 46.0 reduce-scatter.13
where the time goes:
time: 1540 us
  waiting for transfers between devices  702 us (46%)
  matrix products  287 us (19%)
  blocking collectives  242 us (16%)
  local copies, waits for them, and re-layouts  155 us (10%)
  other arithmetic  116 us (8%)
  starting transfers between devices  19.9 us (1%)
  between operations  16.5 us (1%)
    psum x1, waiting for transfers between devices, local(): mixed = lax.psum(mixed_part.astype(jnp.bfloat16), 'tp').astype(jnp.float32)  144 us
    all_gather x1, blocking collectives, local(): lax.all_gather(mix_weight, ('shard', 'ctx'), axis=0, tiled=True)  86.6 us
    psum x1, waiting for transfers between devices, local(): lax.psum((normed2_part + expert_tok_grad).astype(jnp.bfloat16), 'tp')  83.1 us
    all_to_all x1, blocking collectives, local(): lax.all_to_all(pack_rows(expert_grad), ('shard', 'ctx'), split_axis=0, co...  76.7 us
    all_to_all x1, waiting for transfers between devices, local(): lax.all_to_all(pack_rows(normed2_low), ('shard', 'ctx'), split_axis=0, co...  66.5 us
    all_to_all x1, waiting for transfers between devices, local(): lax.all_to_all(unfold_rows(expert_in_grad).astype(jnp.bfloat16), ('shard'...  62.3 us
    psum x1, waiting for transfers between devices, local(): lax.psum(branch_part.astype(jnp.bfloat16), 'tp').astype(jnp.float32)  59.8 us
    reduce_scatter x1, waiting for transfers between devices, local(): lax.psum_scatter(up_grad, ('shard', 'ctx'), scatter_dimension=0, tiled=True)  55.1 us
  transfers between devices with their start and end apart: 19, of which 15 were waited for; matrix products, arithmetic and copies ran while one was open for 13% of the time, Pallas kernels for 0%

commit v1 on v0

--- a/solution.py
+++ b/solution.py
@@ -1,10 +1,13 @@
 import jax
 import jax.numpy as jnp
 from jax import lax
+from jax.experimental import pallas as pl
+from jax.experimental.pallas import tpu as pltpu
 from jax.sharding import PartitionSpec as P
 
 HD = 64
 CAP = 1152
+TILE = 512
 
 
 empty_mark = 1 << 30
@@ -33,6 +36,165 @@
         inverse * (shaped - first_term - unit_rows * second_term),
         jnp.sum(upstream * unit_rows, axis=0),
     )
+
+NT = (((1,), (1,)), ((), ()))
+
+
+def tile_of(index, chunk):
+    per = chunk // TILE
+    return index // per, pl.ds(pl.multiple_of((index % per) * TILE, TILE), TILE)
+
+
+def rows_of(index):
+    return pl.ds(pl.multiple_of(index * TILE, TILE), TILE)
+
+
+def causal():
+    key_at = lax.broadcasted_iota(jnp.int32, (TILE, TILE), 0)
+    query_at = lax.broadcasted_iota(jnp.int32, (TILE, TILE), 1)
+    return key_at <= query_at
+
+
+def flash_forward_body(qkv_ref, out_ref, wide_ref, lse_ref, key_rows):
+    chunks, _, _, chunk = qkv_ref.shape
+    tiles = chunks * chunk // TILE
+    for c in range(chunks):
+        key_rows[pl.ds(c * chunk, chunk), :] = qkv_ref[c, 1].T
+
+    @pl.loop(0, tiles)
+    def _(i):
+        c, at = tile_of(i, chunk)
+        query = qkv_ref[c, 0, :, at] * (HD ** (-0.5))
+
+        def step(j, state, mask):
+            top, total, acc = state
+            kc, kat = tile_of(j, chunk)
+            scores = jnp.dot(key_rows[rows_of(j), :], query, preferred_element_type=jnp.float32)
+            if mask:
+                scores = jnp.where(causal(), scores, masked_score)
+            new_top = jnp.maximum(top, jnp.max(scores, axis=0, keepdims=True))
+            shrink = jnp.exp(top - new_top)
+            weights = jnp.exp(scores - new_top)
+            total = total * shrink + jnp.sum(weights, axis=0, keepdims=True)
+            acc = acc * shrink + jnp.dot(
+                qkv_ref[kc, 2, :, kat],
+                weights.astype(jnp.bfloat16),
+                preferred_element_type=jnp.float32,
+            )
+            return new_top, total, acc
+
+        state = (
+            jnp.full((1, TILE), masked_score, jnp.float32),
+            jnp.zeros((1, TILE), jnp.float32),
+            jnp.zeros((HD, TILE), jnp.float32),
+        )
+        state = step(i, state, True)
+        top, total, acc = lax.fori_loop(0, i, lambda j, s: step(j, s, False), state)
+        result = acc / total
+        wide_ref[c, :, at] = result
+        out_ref[c, :, at] = result.astype(jnp.bfloat16)
+        lse_ref[c, :, at] = top + jnp.log(total)
+
+
+def flash_forward(qkv):
+    chunks, _, width, chunk = qkv.shape
+    return pl.pallas_call(
+        flash_forward_body,
+        name="flash_forward",
+        out_shape=(
+            jax.ShapeDtypeStruct((chunks, width, chunk), jnp.bfloat16),
+            jax.ShapeDtypeStruct((chunks, width, chunk), jnp.float32),
+            jax.ShapeDtypeStruct((chunks, 1, chunk), jnp.float32),
+        ),
+        scratch_shapes=[pltpu.VMEM((chunks * chunk, width), jnp.bfloat16)],
+        cost_estimate=pl.CostEstimate(
+            flops=2 * (chunks * chunk) ** 2 * width * 4, bytes_accessed=5 << 20, transcendentals=0
+        ),
+        compiler_params=pltpu.CompilerParams(vmem_limit_bytes=40 << 20),
+    )(qkv)
+
+
+def flash_backward_body(
+    qkv_ref, grad_ref, wide_ref, lse_ref, out_ref,
+    query_cols, query_rows, key_rows, value_rows, grad_rows, delta, query_grad,
+):
+    chunks, _, _, chunk = qkv_ref.shape
+    tiles = chunks * chunk // TILE
+    scale = HD ** (-0.5)
+    for c in range(chunks):
+        at = pl.ds(c * chunk, chunk)
+        scaled = qkv_ref[c, 0] * scale
+        query_cols[c] = scaled
+        query_rows[at, :] = scaled.T
+        key_rows[at, :] = qkv_ref[c, 1].T
+        value_rows[at, :] = qkv_ref[c, 2].T
+        grad_rows[at, :] = grad_ref[c].T
+        delta[c] = jnp.sum(
+            grad_ref[c].astype(jnp.float32) * wide_ref[c], axis=0, keepdims=True
+        )
+        query_grad[c] = jnp.zeros((HD, chunk), jnp.float32)
+
+    @pl.loop(0, tiles)
+    def _(j):
+        kc, kat = tile_of(j, chunk)
+        key_tile = key_rows[rows_of(j), :]
+        value_tile = value_rows[rows_of(j), :]
+        key_cols = qkv_ref[kc, 1, :, kat]
+
+        def step(i, state, mask):
+            key_grad, value_grad = state
+            c, at = tile_of(i, chunk)
+            scores = jnp.dot(key_tile, query_cols[c, :, at], preferred_element_type=jnp.float32)
+            probs = jnp.exp(scores - lse_ref[c, :, at])
+            if mask:
+                probs = jnp.where(causal(), probs, 0.0)
+            prob_grad = jnp.dot(value_tile, grad_ref[c, :, at], preferred_element_type=jnp.float32)
+            score_grad = (probs * (prob_grad - delta[c, :, at])).astype(jnp.bfloat16)
+            value_grad += jnp.dot(
+                probs.astype(jnp.bfloat16), grad_rows[rows_of(i), :],
+                preferred_element_type=jnp.float32,
+            )
+            key_grad += jnp.dot(
+                score_grad, query_rows[rows_of(i), :], preferred_element_type=jnp.float32
+            )
+            query_grad[c, :, at] += jnp.dot(
+                key_cols, score_grad, preferred_element_type=jnp.float32
+            )
+            return key_grad, value_grad
+
+        state = (jnp.zeros((TILE, HD), jnp.float32), jnp.zeros((TILE, HD), jnp.float32))
+        state = step(j, state, True)
+        key_grad, value_grad = lax.fori_loop(
+            j + 1, tiles, lambda i, s: step(i, s, False), state
+        )
+        out_ref[kc, 1, :, kat] = key_grad.T.astype(jnp.bfloat16)
+        out_ref[kc, 2, :, kat] = value_grad.T.astype(jnp.bfloat16)
+
+    for c in range(chunks):
+        out_ref[c, 0] = (query_grad[c] * scale).astype(jnp.bfloat16)
+
+
+def flash_backward(qkv, grad, wide, lse):
+    chunks, _, width, chunk = qkv.shape
+    full = chunks * chunk
+    return pl.pallas_call(
+        flash_backward_body,
+        name="flash_backward",
+        out_shape=jax.ShapeDtypeStruct((chunks, 3, width, chunk), jnp.bfloat16),
+        scratch_shapes=[
+            pltpu.VMEM((chunks, width, chunk), jnp.bfloat16),
+            pltpu.VMEM((full, width), jnp.bfloat16),
+            pltpu.VMEM((full, width), jnp.bfloat16),
+            pltpu.VMEM((full, width), jnp.bfloat16),
+            pltpu.VMEM((full, width), jnp.bfloat16),
+            pltpu.VMEM((chunks, 1, chunk), jnp.float32),
+            pltpu.VMEM((chunks, width, chunk), jnp.float32),
+        ],
+        cost_estimate=pl.CostEstimate(
+            flops=2 * full ** 2 * width * 10, bytes_accessed=8 << 20, transcendentals=0
+        ),
+        compiler_params=pltpu.CompilerParams(vmem_limit_bytes=48 << 20),
+    )(qkv, grad, wide, lse)
 
 
 def local(
@@ -58,71 +220,35 @@
     live_mask = positions < lengths[0]
     live_rows = live_mask.astype(jnp.float32)[:, None]
     inputs = tokens[0].astype(jnp.float32)
-    gain_one, qkv_full, proj_full, gain_two, mix_full, up_full, down_full = (
-        lax.all_gather(attn_gain, ("shard", "ctx"), axis=0, tiled=True),
-        lax.all_gather(qkv_weight, ("shard", "ctx"), axis=0, tiled=True),
-        lax.all_gather(proj_weight, ("shard", "ctx"), axis=1, tiled=True),
-        lax.all_gather(ffn_gain, ("shard", "ctx"), axis=0, tiled=True),
-        lax.all_gather(mix_weight, ("shard", "ctx"), axis=0, tiled=True),
-        lax.all_gather(up_weight, ("shard", "ctx"), axis=0, tiled=True),
-        lax.all_gather(down_weight, ("shard", "ctx"), axis=1, tiled=True),
-    )
+    group = ("shard", "ctx")
+    members = lax.axis_size(group)
+    small = jnp.concatenate([attn_gain[None], ffn_gain[None], mix_weight.T], axis=0)
+    small = lax.all_gather(small, group, axis=0)
+    small = jnp.swapaxes(small, 0, 1).reshape(4, model_width)
+    gain_one, gain_two, mix_full = small[0], small[1], small[2:].T
+    qkv_full = lax.all_gather(
+        jnp.swapaxes(qkv_weight, 0, 1), group, axis=1, tiled=True
+    )
+    proj_full = lax.all_gather(proj_weight, group, axis=1, tiled=True)
+    up_full = lax.all_gather(up_weight, group, axis=0, tiled=True)
+    down_full = lax.all_gather(down_weight, group, axis=1, tiled=True)
     gain_one = gain_one.astype(jnp.float32)
     gain_two = gain_two.astype(jnp.float32)
-    local_heads = qkv_full.shape[2] // HD
-    score_scale = HD ** (-0.5)
     normed, unit_one, inverse_one = norm_forward(inputs, gain_one)
     normed_low = normed.astype(jnp.bfloat16)
+    ctx_size = lax.axis_size("ctx")
     projected = jnp.einsum(
-        "td,dcf->tcf", normed_low, qkv_full, preferred_element_type=jnp.float32
+        "cdf,td->cft", qkv_full, normed_low, preferred_element_type=jnp.float32
     ).astype(jnp.bfloat16)
-    queries = projected[:, 0].reshape(seq_dev, local_heads, HD)
-    keys_all, values_all = (
-        lax.all_gather(projected[:, 1], "ctx", axis=0, tiled=True),
-        lax.all_gather(projected[:, 2], "ctx", axis=0, tiled=True),
-    )
-    key_block = min(full_len, 1024)
-    block_count = full_len // key_block
-    key_blocks = keys_all.reshape(block_count, key_block, local_heads, HD)
-    value_blocks = values_all.reshape(block_count, key_block, local_heads, HD)
-    key_places = jnp.arange(full_len, dtype=jnp.int32).reshape(block_count, key_block)
-
-    def allowed(places):
-        return ((places[None, :] <= positions[:, None]) & (places[None, :] < lengths[0]))[None]
-
-    def forward_step(state_now, pieces):
-        running_max, running_sum, weighted = state_now
-        key_rows, value_rows, places = pieces
-        visible = allowed(places)
-        scores = (
-            jnp.einsum("qhd,khd->hqk", queries, key_rows, preferred_element_type=jnp.float32)
-            * score_scale
-        )
-        scores = jnp.where(visible, scores, masked_score)
-        new_max = jnp.maximum(running_max, jnp.max(scores, axis=-1))
-        weights = jnp.where(visible, jnp.exp(scores - new_max[..., None]), 0.0)
-        shrink = jnp.exp(running_max - new_max)
-        running_sum = running_sum * shrink + jnp.sum(weights, axis=-1)
-        weighted = weighted * shrink[..., None] + jnp.einsum(
-            "hqk,khd->hqd",
-            weights.astype(jnp.bfloat16),
-            value_rows,
-            preferred_element_type=jnp.float32,
-        )
-        return ((new_max, running_sum, weighted), None)
-
-    start_state = (
-        jnp.full((local_heads, seq_dev), masked_score, jnp.float32),
-        jnp.zeros((local_heads, seq_dev), jnp.float32),
-        jnp.zeros((local_heads, seq_dev, HD), jnp.float32),
-    )
-    (running_max, running_sum, weighted), _ = lax.scan(
-        forward_step, start_state, (key_blocks, value_blocks, key_places)
-    )
-    log_total = running_max + jnp.log(running_sum)
-    heads_out = weighted / running_sum[..., None]
-    attended_low = jnp.transpose(heads_out, (1, 0, 2)).reshape(seq_dev, -1).astype(jnp.bfloat16)
-    branch_part = jnp.dot(attended_low, proj_full, preferred_element_type=jnp.float32)
+    sent_qkv = jnp.swapaxes(projected.reshape(3, ctx_size, HD, seq_dev), 0, 1)
+    qkv = lax.all_to_all(sent_qkv, "ctx", split_axis=0, concat_axis=0, tiled=True)
+    heads_low, heads_wide, log_total = flash_forward(qkv)
+    attended_low = lax.all_to_all(
+        heads_low, "ctx", split_axis=0, concat_axis=0, tiled=True
+    ).reshape(ctx_size * HD, seq_dev)
+    branch_part = jnp.einsum(
+        "ft,fd->td", attended_low, proj_full, preferred_element_type=jnp.float32
+    )
     branch = lax.psum(branch_part.astype(jnp.bfloat16), "tp").astype(jnp.float32)
     middle = inputs + branch
     normed2, unit_two, inverse_two = norm_forward(middle, gain_two)
@@ -240,75 +366,40 @@
     middle_grad = out_grad + middle_norm_grad
     branch_grad = middle_grad.astype(jnp.bfloat16)
     proj_grad = jnp.einsum(
-        "tf,td->fd", attended_low, branch_grad, preferred_element_type=jnp.float32
+        "ft,td->fd", attended_low, branch_grad, preferred_element_type=jnp.float32
     )
     attended_grad = jnp.einsum(
-        "td,fd->tf", branch_grad, proj_full, preferred_element_type=jnp.float32
+        "fd,td->ft", proj_full, branch_grad, preferred_element_type=jnp.float32
     ).astype(jnp.bfloat16)
-    grad_heads = attended_grad.reshape(seq_dev, local_heads, HD)
-    row_delta = jnp.sum(
-        jnp.transpose(grad_heads, (1, 0, 2)).astype(jnp.float32) * heads_out, axis=-1
-    )
-
-    def backward_step(query_grad, pieces):
-        key_rows, value_rows, places = pieces
-        visible = allowed(places)
-        scores = (
-            jnp.einsum("qhd,khd->hqk", queries, key_rows, preferred_element_type=jnp.float32)
-            * score_scale
-        )
-        probs = jnp.where(visible, jnp.exp(scores - log_total[..., None]), 0.0)
-        prob_grad = jnp.einsum(
-            "qhd,khd->hqk", grad_heads, value_rows, preferred_element_type=jnp.float32
-        )
-        score_grad = (probs * (prob_grad - row_delta[..., None])).astype(jnp.bfloat16)
-        query_grad = query_grad + jnp.einsum(
-            "hqk,khd->qhd", score_grad, key_rows, preferred_element_type=jnp.float32
-        )
-        key_grad = jnp.einsum(
-            "hqk,qhd->khd", score_grad, queries, preferred_element_type=jnp.float32
-        )
-        value_grad = jnp.einsum(
-            "hqk,qhd->khd",
-            probs.astype(jnp.bfloat16),
-            grad_heads,
-            preferred_element_type=jnp.float32,
-        )
-        return (query_grad, (key_grad, value_grad))
-
-    query_grad, (key_grad_blocks, value_grad_blocks) = lax.scan(
-        backward_step,
-        jnp.zeros((seq_dev, local_heads, HD), jnp.float32),
-        (key_blocks, value_blocks, key_places),
-    )
-    key_grad_all = key_grad_blocks.reshape(full_len, -1) * score_scale
-    value_grad_all = value_grad_blocks.reshape(full_len, -1)
-    key_grad_own, value_grad_own = (
-        lax.psum_scatter(
-            key_grad_all.astype(jnp.bfloat16), "ctx", scatter_dimension=0, tiled=True
-        ).astype(jnp.float32),
-        lax.psum_scatter(
-            value_grad_all.astype(jnp.bfloat16), "ctx", scatter_dimension=0, tiled=True
-        ).astype(jnp.float32),
-    )
-    qkv_grad = jnp.stack(
-        [(query_grad * score_scale).reshape(seq_dev, -1), key_grad_own, value_grad_own], axis=1
-    ).astype(jnp.bfloat16)
+    heads_grad = lax.all_to_all(
+        attended_grad.reshape(ctx_size, HD, seq_dev), "ctx", split_axis=0, concat_axis=0, tiled=True
+    )
+    sent_grad = flash_backward(qkv, heads_grad, heads_wide, log_total)
+    qkv_grad = lax.all_to_all(sent_grad, "ctx", split_axis=0, concat_axis=0, tiled=True)
+    qkv_grad = jnp.swapaxes(qkv_grad, 0, 1).reshape(3, ctx_size * HD, seq_dev)
     qkv_grad_full = jnp.einsum(
-        "td,tcf->dcf", normed_low, qkv_grad, preferred_element_type=jnp.float32
-    )
-    normed_part = jnp.einsum("tcf,dcf->td", qkv_grad, qkv_full, preferred_element_type=jnp.float32)
+        "td,cft->cdf", normed_low, qkv_grad, preferred_element_type=jnp.float32
+    )
+    normed_part = jnp.einsum("cft,cdf->td", qkv_grad, qkv_full, preferred_element_type=jnp.float32)
     normed_grad = lax.psum(normed_part.astype(jnp.bfloat16), "tp").astype(jnp.float32)
     input_norm_grad, gain_one_grad = norm_backward(normed_grad, gain_one, unit_one, inverse_one)
     tokens_grad = (middle_grad + input_norm_grad).astype(jnp.bfloat16)[None]
+    def shared(value, axis):
+        return lax.psum_scatter(
+            value.astype(jnp.bfloat16), group, scatter_dimension=axis, tiled=True
+        ).astype(jnp.float32)
+
+    small_grad = jnp.concatenate([gain_one_grad[None], gain_two_grad[None], mix_grad.T], axis=0)
+    small_grad = jnp.swapaxes(small_grad.reshape(4, members, -1), 0, 1)
+    small_grad = lax.psum_scatter(small_grad, group, scatter_dimension=0, tiled=True)[0]
     shares = (
-        lax.psum_scatter(gain_one_grad, ("shard", "ctx"), scatter_dimension=0, tiled=True),
-        lax.psum_scatter(qkv_grad_full, ("shard", "ctx"), scatter_dimension=0, tiled=True),
-        lax.psum_scatter(proj_grad, ("shard", "ctx"), scatter_dimension=1, tiled=True),
-        lax.psum_scatter(gain_two_grad, ("shard", "ctx"), scatter_dimension=0, tiled=True),
-        lax.psum_scatter(mix_grad, ("shard", "ctx"), scatter_dimension=0, tiled=True),
-        lax.psum_scatter(up_grad, ("shard", "ctx"), scatter_dimension=0, tiled=True),
-        lax.psum_scatter(down_grad, ("shard", "ctx"), scatter_dimension=1, tiled=True),
+        small_grad[0],
+        jnp.swapaxes(shared(qkv_grad_full, 1), 0, 1),
+        shared(proj_grad, 1),
+        small_grad[1],
+        small_grad[2:].T,
+        shared(up_grad, 0),
+        shared(down_grad, 1),
     )
     return (
         layer_out,

time: 1540 us -> 1190 us (0.77)
  matrix products: 287 us -> 112 us
  waiting for transfers between devices: 702 us -> 581 us
  blocking collectives: 242 us -> 179 us
  Pallas kernels: 0 us -> 55.8 us
  other arithmetic: 116 us -> 81.7 us
  local copies, waits for them, and re-layouts: 155 us -> 123 us
    reduce_scatter x6 -> x1, waiting for transfers between devices: 224 us -> 0.01 us  [shared(): lax.psum_scatter(value.astype(jnp.bfloat16), group, scatter_dimension=axi...]
    dot_general x34 -> x7, matrix products: 195 us -> 22.7 us  [the longest x1 5.04 us: local(): jnp.einsum('cft,cdf->td', qkv_grad, qkv_full, preferred_element_type=jnp....]
    all_gather x4 -> x2, blocking collectives: 141 us -> 42.6 us  [the longest x1 27.7 us: local(): proj_full = lax.all_gather(proj_weight, group, axis=1, tiled=True)]
    all_to_all x1, waiting for transfers between devices: 0.01 us -> 69.9 us  [local(): lax.all_to_all(unfold_rows(expert_part).astype(jnp.bfloat16), ('shard', '...]
    pallas_call x0 -> x2, Pallas kernels: none -> 55.8 us  [the longest x1 32.2 us: flash_backward(): pl.pallas_call(flash_backward_body, name='flash_backward', out_shape=jax....]
    all_gather x5 -> x3, waiting for transfers between devices: 54 us -> 10 us  [the longest x1 9.99 us: local(): lax.all_gather(jnp.swapaxes(qkv_weight, 0, 1), group, axis=1, tiled=True)]
    unnamed x16 -> x13, waiting for transfers between devices: 7.93 us -> 49 us
    convert_element_type x4 -> x0, local copies, waits for them, and re-layouts: 25.7 us -> none  [the longest x2 13.9 us: local(): value_grad_all.astype(jnp.bfloat16)]
  transfers between devices with their start and end apart: 19 -> 17, of which waited for: 15 -> 11; matrix products, arithmetic and copies ran while one was open for 13% -> 17% of each run, Pallas kernels for 0% -> 3%
where the time goes in v1:
time: 1190 us; the launch traced here: 1180 us
  waiting for transfers between devices  581 us (49%)
  blocking collectives  179 us (15%)
  local copies, waits for them, and re-layouts  123 us (10%)
  matrix products  112 us (9%)
  other arithmetic  81.7 us (7%)
  Pallas kernels  55.8 us (5%)
  starting transfers between devices  31.4 us (3%)
  between operations  15.8 us (1%)
    psum x1, waiting for transfers between devices, local(): mixed = lax.psum(mixed_part.astype(jnp.bfloat16), 'tp').astype(jnp.float32)  156 us
    all_to_all x1, blocking collectives, local(): lax.all_to_all(pack_rows(expert_grad), ('shard', 'ctx'), split_axis=0, co...  76.9 us
    psum x1, waiting for transfers between devices, local(): lax.psum(branch_part.astype(jnp.bfloat16), 'tp').astype(jnp.float32)  74.1 us
    psum x1, waiting for transfers between devices, local(): lax.psum((normed2_part + expert_tok_grad).astype(jnp.bfloat16), 'tp')  72.3 us
    all_to_all x1, waiting for transfers between devices, local(): lax.all_to_all(unfold_rows(expert_part).astype(jnp.bfloat16), ('shard', '...  69.9 us
    all_to_all x1, waiting for transfers between devices, local(): lax.all_to_all(pack_rows(normed2_low), ('shard', 'ctx'), split_axis=0, co...  66.4 us
    all_to_all x1, waiting for transfers between devices, local(): lax.all_to_all(unfold_rows(expert_in_grad).astype(jnp.bfloat16), ('shard'...  62.5 us
    unnamed x13, waiting for transfers between devices  49 us
  transfers between devices with their start and end apart: 17, of which 11 were waited for; matrix products, arithmetic and copies ran while one was open for 17% of the time, Pallas kernels for 3%

profile of v1, /device:TPU:0, one launch (start us, length us, event | category | flops | bytes accessed | tf_op | source)
XLA Modules:
  0.0 1180.1 jit_solution(1923838027302523645)
XLA Ops:
  9.8 14.9 %all-gather.1 = bf16[8,4,128]{2,1,0:T(4,128)(2,1)S(1)} all-gather(bf16[1,4,128]{2,1,0:T(4,128)(2,1)S(1)} %maximum_bitcast_fusion.1), channel_id=2, replica_groups=mesh['shard'=2,'ctx'=4,'tp'=4] {'shard','ctx'}, dimensions={0}, use_global_device_ids=true | all-gather | bytes 9216 | tf_op jit(solution)/shard_map/all_gather | solution.py:226
  29.0 10.0 all-gather.6.cloned.1.call-done
  43.2 22.9 %all_to_all.49.qkv_ref = bf16[4,3,64,1024]{3,2,1,0:T(8,128)(2,1)S(1)} all-to-all(bf16[4,3,64,1024]{3,2,1,0:T(8,128)(2,1)S(1)} %bitcast.250), channel_id=1, replica_groups=mesh['shard'=2,'ctx'=4,'tp'=4] {'ctx'}, dimensions={0} | all-to-all | bytes 3145728 | tf_op jit(solution)/shard_map/all_to_all | solution.py:244
  66.1 23.6 %flash_forward.1 = (bf16[4,64,1024]{2,1,0:T(8,128)(2,1)}, f32[4,64,1024]{2,1,0:T(8,128)S(1)}, f32[4,1,1024]{2,1,0:T(1,128)S(1)}) custom-call(bf16[4,3,64,1024]{3,2,1,0:T(8,128)(2,1)S(1)} %all_to_all.49.qkv_ref), custom_call_target="tpu_custom_call" | custom-call | flops 8589934592 | bytes 5242880 | tf_op jit(solution)/shard_map/flash_forward/pallas_call | solution.py:101
  94.1 27.7 %all_gather.21 = bf16[256,1024]{1,0:T(8,128)(2,1)} all-gather(bf16[256,128]{1,0:T(8,128)(2,1)S(1)} %copy-done.17), channel_id=1, replica_groups=mesh['shard'=2,'ctx'=4,'tp'=4] {'shard','ctx'}, dimensions={1}, use_global_device_ids=true | all-gather | bytes 589824 | tf_op jit(solution)/shard_map/all_gather | solution.py:232
  137.2 74.1 %all-reduce.6.cloned.1.call-done = bf16[1024,1024]{1,0:T(8,128)(2,1)} async-done(((bf16[1024,1024]{1,0:T(8,128)(2,1)}), bf16[1024,1024]{1,0:T(8,128)(2,1)}) %all-reduce.6.cloned.1.call-update) | async-done | bytes 2097168 | tf_op jit(solution)/shard_map/psum | solution.py:252
  217.9 9.8 scatter_custom_fusion.1
  245.4 66.4 %all-to-all-done.3 = bf16[8,384,1024]{2,1,0:T(8,128)(2,1)} async-done(((bf16[8,384,1024]{2,1,0:T(8,128)(2,1)}), bf16[8,384,1024]{2,1,0:T(8,128)(2,1)}, u32[]{:S(2)}, u32[]{:S(2)}) %all-to-all-start.3) | async-done | bytes 6291488 | tf_op jit(solution)/shard_map/all_to_all | solution.py:285
  311.8 10.2 gather_fusion
  333.7 14.5 %scatter_custom_fusion.2 = f32[3072,1024]{1,0:T(8,128)} fusion(s32[1152]{0:T(1024)S(1)} %compare_select_fusion.2, f32[1152,1024]{1,0:T(8,128)} %convolution_multiply_fusion, f32[]{:T(128)} %constant.19.clone.1), kind=kCustom, calls=%fused_computation.16 | custom fusion | bytes 12583424 | tf_op jit(solution)/shard_map/scatter | solution.py:308
  348.3 8.2 convert_element_type.187
  370.7 69.9 %all-to-all-done.4 = bf16[8,384,1024]{2,1,0:T(8,128)(2,1)} async-done(((bf16[8,384,1024]{2,1,0:T(8,128)(2,1)}), bf16[8,384,1024]{2,1,0:T(8,128)(2,1)}, u32[]{:S(2)}, u32[]{:S(2)}) %all-to-all-start.4) | async-done | bytes 6291488 | tf_op jit(solution)/shard_map/all_to_all | solution.py:311
  440.6 8.9 bitcast_convert_fusion.1
  449.5 10.9 gather_fusion.2
  460.4 9.5 fusion.45
  470.0 10.0 psum.38
  480.1 10.1 scatter_custom_fusion.3
  490.1 76.9 %all_to_all.50 = bf16[8,384,1024]{2,1,0:T(8,128)(2,1)} all-to-all(bf16[8,384,1024]{2,1,0:T(8,128)(2,1)} %bitcast.244), channel_id=1, replica_groups=mesh['shard'=2,'ctx'=4,'tp'=4] {'shard','ctx'}, dimensions={0} | all-to-all | bytes 12582912 | tf_op jit(solution)/shard_map/all_to_all | solution.py:334
  567.0 10.2 gather_fusion.3
  590.9 14.3 %scatter_custom_fusion.4 = f32[3072,1024]{1,0:T(8,128)} fusion(s32[1152]{0:T(1024)S(1)} %compare_select_fusion.2, f32[1152,1024]{1,0:T(8,128)} %fusion.67, f32[]{:T(128)} %constant.19.clone.1), kind=kCustom, calls=%fused_computation.14 | custom fusion | bytes 12583424 | tf_op jit(solution)/shard_map/scatter | solution.py:308
  605.3 8.2 convert_element_type.199
  618.6 8.2 fusion.34
  626.8 62.5 %all-to-all-done.6 = bf16[8,384,1024]{2,1,0:T(8,128)(2,1)} async-done(((bf16[8,384,1024]{2,1,0:T(8,128)(2,1)}), bf16[8,384,1024]{2,1,0:T(8,128)(2,1)}, u32[]{:S(2)}, u32[]{:S(2)}) %all-to-all-start.6) | async-done | bytes 6291488 | tf_op jit(solution)/shard_map/all_to_all | solution.py:346
  689.3 8.9 bitcast_convert_fusion
  698.2 11.0 gather_fusion.4
  727.4 72.3 %all-reduce.8.cloned.1.call-done = bf16[1024,1024]{1,0:T(8,128)(2,1)} async-done(((bf16[1024,1024]{1,0:T(8,128)(2,1)}), bf16[1024,1024]{1,0:T(8,128)(2,1)}) %all-reduce.8.cloned.1.call-update) | async-done | bytes 2097168 | tf_op jit(solution)/shard_map/psum | solution.py:355
  824.7 32.2 %flash_backward.1 = bf16[4,3,64,1024]{3,2,1,0:T(8,128)(2,1)} custom-call(bf16[4,3,64,1024]{3,2,1,0:T(8,128)(2,1)S(1)} %copy-done.3, bf16[4,64,1024]{2,1,0:T(8,128)(2,1)S(1)} %all-to-all-done.7.grad_ref, f32[4,64,1024]{2,1,0:T(8,128)S(1)} %get-tuple-element.17.wide_ref, f32[4,1,1024]{2,1,0:T(1,128)S(1)} %get-tuple-element.18.lse_ref), custom_call_target="tpu_custom_call" | custom-call | flops 21474836480 | bytes 8388608 | tf_op jit(solution)/shard_map/flash_backward/pallas_call | solution.py:180
  865.8 19.5 %all-to-all-done.8 = bf16[4,3,64,1024]{3,2,1,0:T(8,128)(2,1)} async-done(((bf16[4,3,64,1024]{3,2,1,0:T(8,128)(2,1)}), bf16[4,3,64,1024]{3,2,1,0:T(8,128)(2,1)}, u32[]{:S(2)}, u32[]{:S(2)}) %all-to-all-start.8) | async-done | bytes 1572896 | tf_op jit(solution)/shard_map/all_to_all | solution.py:378
  926.4 8.0 reduce-scatter.15.cloned.1.call-done
  936.0 40.0 %reduce-scatter.13.cloned.1.call-done = bf16[128,768]{1,0:T(8,128)(2,1)} async-done(((bf16[1024,768]{1,0:T(8,128)(2,1)}), bf16[128,768]{1,0:T(8,128)(2,1)}) %reduce-scatter.13.cloned.1.call-update) | async-done | bytes 196624
  978.3 155.7 %all-reduce.10.cloned.1.call-done = (bf16[1024,1024]{1,0:T(8,128)(2,1)}, bf16[1024,1024]{1,0:T(8,128)(2,1)}) async-done(((bf16[1024,1024]{1,0:T(8,128)(2,1)}, bf16[1024,1024]{1,0:T(8,128)(2,1)}), (bf16[1024,1024]{1,0:T(8,128)(2,1)}, bf16[1024,1024]{1,0:T(8,128)(2,1)})) %all-reduce.10.cloned.1.call-update) | async-done | bytes 4194320 | tf_op jit(solution)/shard_map/psum | solution.py:320
  1137.5 26.5 %all-reduce = f32[8,4,128]{2,1,0:T(4,128)S(1)} all-reduce(f32[8,4,128]{2,1,0:T(4,128)S(1)} %maximum_bitcast_fusion), channel_id=3, replica_groups=mesh['shard'=2,'ctx'=4,'tp'=4] {'shard','ctx'}, use_global_device_ids=true, to_apply=%region_29.30.clone | all-reduce | flops 4096 | bytes 32768
  (184 shorter events, 208.3 us)
Async XLA Ops:
  7.2 321.9 %copy-start = (bf16[1,1024,1024]{2,1,0:T(8,128)(2,1)S(1)}, bf16[1,1024,1024]{2,1,0:T(8,128)(2,1)}, u32[]{:S(2)}) copy-start(bf16[1,1024,1024]{2,1,0:T(8,128)(2,1)} %param.26) | copy-start | bytes 6291460
  7.2 31.8 %all-gather.6.cloned.1.call-start = ((), (), s32[]{:S(2)}) async-start(), calls=%async_computation.13 | async-start | bytes 1769472 | tf_op jit(solution)/shard_map/all_gather | solution.py:229
  26.7 16.4 %copy-start.18 = (f32[1024]{0:T(1024)}, f32[1024]{0:T(1024)S(1)}, u32[]{:S(2)}) copy-start(f32[1024]{0:T(1024)S(1)} %broadcast_multiply_fusion.5) | copy-start | bytes 12292
  29.0 14.1 %copy-start.23 = (f32[1024]{0:T(1024)}, f32[1024]{0:T(1024)S(1)}, u32[]{:S(2)}) copy-start(f32[1024]{0:T(1024)S(1)} %add_rsqrt_fusion.1) | copy-start | bytes 12292
  29.0 186.7 %copy-start.29 = (f32[1,8,128]{2,0,1:T(1,128)}, f32[1,8,128]{2,0,1:T(1,128)S(1)}, u32[]{:S(2)}) copy-start(f32[1,8,128]{2,0,1:T(1,128)S(1)} %get-tuple-element.71) | copy-start | bytes 12292
  66.1 23.6 %copy-start.2 = (bf16[4,3,64,1024]{3,2,1,0:T(8,128)(2,1)}, bf16[4,3,64,1024]{3,2,1,0:T(8,128)(2,1)S(1)}, u32[]{:S(2)}) copy-start(bf16[4,3,64,1024]{3,2,1,0:T(8,128)(2,1)S(1)} %all_to_all.49.qkv_ref) | copy-start | bytes 4718596
  66.1 27.9 %copy-start.17 = (bf16[256,128]{1,0:T(8,128)(2,1)S(1)}, bf16[256,128]{1,0:T(8,128)(2,1)}, u32[]{:S(2)}) copy-start(bf16[256,128]{1,0:T(8,128)(2,1)} %param.20) | copy-start | bytes 196612
  89.7 36.0 %copy-start.22 = (s32[1,1024,1]{1,2,0:T(1,128)S(1)}, s32[1,1024,1]{1,2,0:T(1,128)}, u32[]{:S(2)}) copy-start(s32[1,1024,1]{1,2,0:T(1,128)} %param.16) | copy-start | bytes 12292
  89.7 32.0 %all-to-all-start.1 = ((bf16[4,64,1024]{2,1,0:T(8,128)(2,1)}), bf16[4,64,1024]{2,1,0:T(8,128)(2,1)}, u32[]{:S(2)}, u32[]{:S(2)}) async-start(bf16[4,64,1024]{2,1,0:T(8,128)(2,1)} %get-tuple-element.15), calls=%async_computation.1 | async-start | bytes 1048576 | tf_op jit(solution)/shard_map/all_to_all | solution.py:246
  94.0 117.2 %all-reduce.6.cloned.1.call-start = ((), (), s32[]{:S(2)}) async-start(), calls=%async_computation.14 | async-start | bytes 4194304 | tf_op jit(solution)/shard_map/psum | solution.py:252
  133.6 94.0 %all-to-all-start.2 = ((s32[8,1,384]{2,1,0:T(1,128)}), s32[8,1,384]{2,1,0:T(1,128)S(1)}, u32[]{:S(2)}, u32[]{:S(2)}) async-start(s32[8,1,384]{2,1,0:T(1,128)} %bitcast.25), calls=%async_computation.2 | async-start | bytes 24576 | tf_op jit(solution)/shard_map/all_to_all | solution.py:288
  227.7 84.1 %all-to-all-start.3 = ((bf16[8,384,1024]{2,1,0:T(8,128)(2,1)}), bf16[8,384,1024]{2,1,0:T(8,128)(2,1)}, u32[]{:S(2)}, u32[]{:S(2)}) async-start(bf16[8,384,1024]{2,1,0:T(8,128)(2,1)} %bitcast.243), calls=%async_computation.3 | async-start | bytes 12582912 | tf_op jit(solution)/shard_map/all_to_all | solution.py:285
  232.4 131.7 %all-gather.8.cloned.1.call-start = ((), (), s32[]{:S(2)}) async-start(), calls=%async_computation.15 | async-start | bytes 2359296 | tf_op jit(solution)/shard_map/all_gather | solution.py:233
  356.4 84.2 %all-to-all-start.4 = ((bf16[8,384,1024]{2,1,0:T(8,128)(2,1)}), bf16[8,384,1024]{2,1,0:T(8,128)(2,1)}, u32[]{:S(2)}, u32[]{:S(2)}) async-start(bf16[8,384,1024]{2,1,0:T(8,128)(2,1)} %bitcast.245), calls=%async_computation.4 | async-start | bytes 12582912 | tf_op jit(solution)/shard_map/all_to_all | solution.py:311
  361.2 99.2 %all-gather.10.cloned.1.call-start = ((), (), s32[]{:S(2)}) async-start(), calls=%async_computation.16 | async-start | bytes 2359296 | tf_op jit(solution)/shard_map/all_gather | solution.py:234
  613.4 75.9 %all-to-all-start.6 = ((bf16[8,384,1024]{2,1,0:T(8,128)(2,1)}), bf16[8,384,1024]{2,1,0:T(8,128)(2,1)}, u32[]{:S(2)}, u32[]{:S(2)}) async-start(bf16[8,384,1024]{2,1,0:T(8,128)(2,1)} %bitcast.246), calls=%async_computation.6 | async-start | bytes 12582912 | tf_op jit(solution)/shard_map/all_to_all | solution.py:346
  618.4 181.3 %all-reduce.8.cloned.1.call-start = ((), (), s32[]{:S(2)}) async-start(), calls=%async_computation.17 | async-start | bytes 4194304 | tf_op jit(solution)/shard_map/psum | solution.py:355
  716.4 190.9 %reduce-scatter.17.cloned.1.call-start = ((), (), s32[]{:S(2)}) async-start(), calls=%async_computation.21 | async-start | bytes 2359296
  723.2 76.4 %copy-start.5 = (bf16[1,1024,1024]{2,1,0:T(8,128)(2,1)S(1)}, bf16[1,1024,1024]{2,1,0:T(8,128)(2,1)}, u32[]{:S(2)}) copy-start(bf16[1,1024,1024]{2,1,0:T(8,128)(2,1)} %param.14) | copy-start | bytes 6291460
  723.2 76.4 %copy-start.21 = (f32[1024]{0:T(1024)S(1)}, f32[1024]{0:T(1024)}, u32[]{:S(2)}) copy-start(f32[1024]{0:T(1024)} %copy-done.20) | copy-start | bytes 12292
  723.2 76.4 %copy-start.26 = (f32[1024]{0:T(1024)S(1)}, f32[1024]{0:T(1024)}, u32[]{:S(2)}) copy-start(f32[1024]{0:T(1024)} %copy-done.25) | copy-start | bytes 12292
  723.2 76.4 %copy-start.30 = (f32[1,8,128]{2,0,1:T(1,128)S(1)}, f32[1,8,128]{2,0,1:T(1,128)}, u32[]{:S(2)}) copy-start(f32[1,8,128]{2,0,1:T(1,128)} %copy-done.29) | copy-start | bytes 12292
  813.2 11.4 all-to-all-start.7
  816.9 92.4 %reduce-scatter.11.cloned.1.call-start = ((), (), s32[]{:S(2)}) async-start(), calls=%async_computation.18 | async-start | bytes 2359296 | tf_op jit(solution)/shard_map/reduce_scatter | solution.py:388
  856.9 28.5 %all-to-all-start.8 = ((bf16[4,3,64,1024]{3,2,1,0:T(8,128)(2,1)}), bf16[4,3,64,1024]{3,2,1,0:T(8,128)(2,1)}, u32[]{:S(2)}, u32[]{:S(2)}) async-start(bf16[4,3,64,1024]{3,2,1,0:T(8,128)(2,1)} %flash_backward.1), calls=%async_computation.8 | async-start | bytes 3145728 | tf_op jit(solution)/shard_map/all_to_all | solution.py:378
  861.5 26.6 %copy-start.6 = (bf16[1,1024,1024]{2,1,0:T(8,128)(2,1)S(1)}, bf16[1,1024,1024]{2,1,0:T(8,128)(2,1)}, u32[]{:S(2)}) copy-start(bf16[1,1024,1024]{2,1,0:T(8,128)(2,1)} %param.14) | copy-start | bytes 6291460
  861.5 26.6 %copy-start.19 = (f32[1024]{0:T(1024)S(1)}, f32[1024]{0:T(1024)}, u32[]{:S(2)}) copy-start(f32[1024]{0:T(1024)} %copy-done.18) | copy-start | bytes 12292
  861.5 26.6 %copy-start.24 = (f32[1024]{0:T(1024)S(1)}, f32[1024]{0:T(1024)}, u32[]{:S(2)}) copy-start(f32[1024]{0:T(1024)} %copy-done.23) | copy-start | bytes 12292
  861.5 26.6 %copy-start.28 = (f32[1,8,128]{2,0,1:T(1,128)S(1)}, f32[1,8,128]{2,0,1:T(1,128)}, u32[]{:S(2)}) copy-start(f32[1,8,128]{2,0,1:T(1,128)} %copy-done.27) | copy-start | bytes 12292
  861.5 72.9 %reduce-scatter.15.cloned.1.call-start = ((), (), s32[]{:S(2)}) async-start(), calls=%async_computation.20 | async-start | bytes 589824
  865.8 110.3 %reduce-scatter.13.cloned.1.call-start = ((), (), s32[]{:S(2)}) async-start(), calls=%async_computation.19 | async-start | bytes 1769472
  898.5 235.5 %all-reduce.10.cloned.1.call-start = ((), (), s32[]{:S(2)}) async-start(), calls=%async_computation.22 | async-start | bytes 8388608 | tf_op jit(solution)/shard_map/psum | solution.py:320
  (20 other events, 110.3 us)
Sparse Core Ops, SparseCore 0:
  10.5 28.4 all-gather.5
  125.2 86.0 all-reduce.5
  235.1 59.4 all-gather.7
  363.6 60.1 all-gather.9
  716.6 83.0 all-reduce.7
  803.3 40.1 reduce-scatter.16
  847.4 49.7 reduce-scatter.10
  900.2 34.1 reduce-scatter.14
  937.7 38.3 reduce-scatter.12
  978.9 155.0 all-reduce.9

commit v2 on v1

--- a/solution.py
+++ b/solution.py
@@ -222,10 +222,44 @@
     inputs = tokens[0].astype(jnp.float32)
     group = ("shard", "ctx")
     members = lax.axis_size(group)
-    small = jnp.concatenate([attn_gain[None], ffn_gain[None], mix_weight.T], axis=0)
+    tokens_total = members * seq_dev
+    code = jnp.where(
+        live_mask, routes[0, :, 0] * tokens_total + priority[0], members * tokens_total
+    )
+    small = [attn_gain[None], ffn_gain[None], mix_weight.T]
+    small = jnp.concatenate(small, axis=0).astype(jnp.float32)
+    small_width = small.shape[1]
+    small = jnp.concatenate([small.reshape(-1), code.astype(jnp.float32)])
     small = lax.all_gather(small, group, axis=0)
-    small = jnp.swapaxes(small, 0, 1).reshape(4, model_width)
-    gain_one, gain_two, mix_full = small[0], small[1], small[2:].T
+    code_all = small[:, 4 * small_width :].reshape(-1).astype(jnp.int32)
+    small = jnp.swapaxes(small[:, : 4 * small_width].reshape(members, 4, small_width), 0, 1)
+    small = small.reshape(4, model_width)
+    gain_one, gain_two, mix_full = small[0], small[1], small[2:].T.astype(jnp.bfloat16)
+    own_code = code_all - lax.axis_index(group) * tokens_total
+    mine = (own_code >= 0) & (own_code < tokens_total)
+    sorted_code, ranking = lax.sort(
+        (
+            jnp.where(mine, own_code, empty_mark),
+            lax.iota(jnp.int32, tokens_total),
+        ),
+        num_keys=1,
+    )
+    ranking = ranking[:CAP]
+    taken = sorted_code[:CAP] < empty_mark
+    taken_mask = taken.astype(jnp.float32)[:, None]
+    place = jnp.where(taken, ranking, tokens_total)
+    part_width = model_width // lax.axis_size("tp")
+
+    def columns(value):
+        return lax.dynamic_slice_in_dim(
+            value, lax.axis_index("tp") * part_width, part_width, axis=1
+        )
+
+    def rows_for_expert(value):
+        everyone = lax.all_gather(columns(value), group, axis=0, tiled=True)
+        return lax.all_gather(everyone[ranking], "tp", axis=1, tiled=True)
+
+    grad_rows = rows_for_expert(cotangent[0])
     qkv_full = lax.all_gather(
         jnp.swapaxes(qkv_weight, 0, 1), group, axis=1, tiled=True
     )
@@ -259,82 +293,34 @@
     upper_pre = jnp.dot(normed2_low, up_full, preferred_element_type=jnp.float32)
     hidden_low = gelu_tanh(upper_pre).astype(jnp.bfloat16)
     dense_part = jnp.dot(hidden_low, down_full, preferred_element_type=jnp.float32)
-    experts_total = lax.axis_size(("shard", "ctx"))
-    slot_cap = max(4, 3 * seq_dev // experts_total)
-    chosen = routes[0, :, 0]
-    onehot = (chosen[:, None] == jnp.arange(experts_total, dtype=jnp.int32)[None, :]).astype(
-        jnp.int32
-    )
-    slot_pos = jnp.sum(jnp.cumsum(onehot, axis=0) * onehot, axis=1) - 1
-    target = jnp.where(live_mask, chosen * slot_cap + slot_pos, experts_total * slot_cap)
-
-    def pack_rows(token_rows):
-        buffer = jnp.zeros((experts_total * slot_cap, model_width), token_rows.dtype)
-        return (
-            buffer.at[target]
-            .set(token_rows, mode="drop")
-            .reshape(experts_total, slot_cap, model_width)
-        )
-
-    send_order = (
-        jnp.full((experts_total * slot_cap,), empty_mark, jnp.int32)
-        .at[target]
-        .set(priority[0], mode="drop")
-    )
-    recv_rows, recv_order = (
-        lax.all_to_all(
-            pack_rows(normed2_low), ("shard", "ctx"), split_axis=0, concat_axis=0, tiled=True
-        ),
-        lax.all_to_all(
-            send_order.reshape(experts_total, slot_cap),
-            ("shard", "ctx"),
-            split_axis=0,
-            concat_axis=0,
-            tiled=True,
-        ),
-    )
-    flat_order = recv_order.reshape(-1)
-    ranking = jnp.argsort(flat_order)[:CAP]
-    taken_mask = (flat_order[ranking] < empty_mark).astype(jnp.float32)[:, None]
-    expert_in = recv_rows.reshape(-1, model_width)[ranking]
     own_up = expert_up[0]
     own_down = expert_down[0]
+    expert_in = rows_for_expert(normed2_low)
+    expert_mixing = jax.nn.softmax(
+        jnp.dot(expert_in, mix_full, preferred_element_type=jnp.float32), axis=-1
+    )
+    grad_in = (expert_mixing[:, 1:2] * grad_rows.astype(jnp.float32) * taken_mask).astype(
+        jnp.bfloat16
+    )
     expert_pre = jnp.dot(expert_in, own_up, preferred_element_type=jnp.float32)
     expert_hidden = gelu_tanh(expert_pre).astype(jnp.bfloat16)
-    expert_part = jnp.dot(expert_hidden, own_down, preferred_element_type=jnp.float32) * taken_mask
-
-    def unfold_rows(slot_rows):
-        buffer = jnp.zeros((experts_total * slot_cap, model_width), jnp.float32)
-        return buffer.at[ranking].set(slot_rows).reshape(experts_total, slot_cap, model_width)
-
-    full_index = jnp.where(live_mask, chosen * slot_cap + slot_pos, 0)
-    returned_rows = lax.all_to_all(
-        unfold_rows(expert_part).astype(jnp.bfloat16),
-        ("shard", "ctx"),
-        split_axis=0,
-        concat_axis=0,
-        tiled=True,
-    ).astype(jnp.float32)
-    expert_tok = returned_rows.reshape(-1, model_width)[full_index] * live_rows
-    mixed_part = mixing[:, 0:1] * dense_part + mixing[:, 1:2] * expert_tok
-    mixed = lax.psum(mixed_part.astype(jnp.bfloat16), "tp").astype(jnp.float32)
-    layer_out = ((middle + mixed) * live_rows).astype(jnp.bfloat16)[None]
+    expert_part = jnp.dot(expert_hidden, own_down, preferred_element_type=jnp.float32)
+
+    def summed_columns(value):
+        return lax.psum_scatter(
+            value.astype(jnp.bfloat16), "tp", scatter_dimension=1, tiled=True
+        )
+
     out_grad = cotangent[0].astype(jnp.float32) * live_rows
     dense_grad = (mixing[:, 0:1] * out_grad).astype(jnp.bfloat16)
-    expert_grad = (mixing[:, 1:2] * out_grad).astype(jnp.bfloat16)
-    dots_part = jnp.stack(
-        [jnp.sum(out_grad * dense_part, axis=-1), jnp.sum(out_grad * expert_tok, axis=-1)], axis=-1
-    )
+    dense_cols = summed_columns(dense_part).astype(jnp.float32)
+    expert_cols = summed_columns(expert_part)
     down_grad = jnp.einsum("tf,td->fd", hidden_low, dense_grad, preferred_element_type=jnp.float32)
     hidden_grad = jnp.einsum("td,fd->tf", dense_grad, down_full, preferred_element_type=jnp.float32)
     _, gelu_pull = jax.vjp(gelu_tanh, upper_pre)
     upper_grad = gelu_pull(hidden_grad)[0].astype(jnp.bfloat16)
     up_grad = jnp.einsum("td,tf->df", normed2_low, upper_grad, preferred_element_type=jnp.float32)
     normed2_part = jnp.einsum("tf,df->td", upper_grad, up_full, preferred_element_type=jnp.float32)
-    recv_grad = lax.all_to_all(
-        pack_rows(expert_grad), ("shard", "ctx"), split_axis=0, concat_axis=0, tiled=True
-    )
-    grad_in = recv_grad.reshape(-1, model_width)[ranking]
     own_down_grad = jnp.einsum(
         "cf,cd->fd", expert_hidden, grad_in, preferred_element_type=jnp.float32
     )
@@ -343,18 +329,27 @@
     epre_grad = expert_pull(ehidden_grad)[0].astype(jnp.bfloat16)
     own_up_grad = jnp.einsum("cd,cf->df", expert_in, epre_grad, preferred_element_type=jnp.float32)
     expert_in_grad = jnp.einsum("cf,df->cd", epre_grad, own_up, preferred_element_type=jnp.float32)
-    sent_back = lax.all_to_all(
-        unfold_rows(expert_in_grad).astype(jnp.bfloat16),
-        ("shard", "ctx"),
-        split_axis=0,
-        concat_axis=0,
-        tiled=True,
-    ).astype(jnp.float32)
-    expert_tok_grad = sent_back.reshape(-1, model_width)[full_index] * live_rows
-    normed2_grad, branch_dots = (
-        lax.psum((normed2_part + expert_tok_grad).astype(jnp.bfloat16), "tp").astype(jnp.float32),
-        lax.psum(dots_part.astype(jnp.bfloat16), "tp").astype(jnp.float32),
-    )
+    grad_cols = summed_columns(expert_in_grad)
+    normed2_cols = summed_columns(normed2_part).astype(jnp.float32)
+    placed = (
+        jnp.zeros((tokens_total, 2 * part_width), jnp.bfloat16)
+        .at[place]
+        .set(jnp.concatenate([expert_cols, grad_cols], axis=1), mode="drop", unique_indices=True)
+    )
+    returned = lax.psum_scatter(placed, group, scatter_dimension=0, tiled=True).astype(jnp.float32)
+    expert_tok = returned[:, :part_width]
+    mixed = mixing[:, 0:1] * dense_cols + mixing[:, 1:2] * expert_tok
+    out_cols = ((columns(middle) + mixed) * live_rows).astype(jnp.bfloat16)
+    layer_out = lax.all_gather(out_cols, "tp", axis=1, tiled=True)[None]
+    grad_part = columns(out_grad)
+    dots_part = jnp.stack(
+        [jnp.sum(grad_part * dense_cols, axis=-1), jnp.sum(grad_part * expert_tok, axis=-1)]
+    ).reshape(-1, part_width)
+    normed2_cols = jnp.concatenate([normed2_cols + returned[:, part_width:], dots_part], axis=0)
+    gathered = lax.all_gather(normed2_cols.astype(jnp.bfloat16), "tp", axis=0)
+    gathered = gathered.astype(jnp.float32)
+    normed2_grad = jnp.swapaxes(gathered[:, :seq_dev], 0, 1).reshape(seq_dev, model_width)
+    branch_dots = jnp.sum(gathered[:, seq_dev:], axis=0).reshape(2, seq_dev).T
     logit_grad = mixing * (branch_dots - jnp.sum(mixing * branch_dots, axis=-1, keepdims=True))
     mix_grad = jnp.dot(
         normed2_low.astype(jnp.float32).T, logit_grad, precision=lax.Precision.HIGHEST

time: 1190 us -> 1100 us (0.924)
  waiting for transfers between devices: 581 us -> 654 us
  local copies, waits for them, and re-layouts: 123 us -> 65.4 us
  blocking collectives: 179 us -> 126 us
  starting transfers between devices: 31.4 us -> 9.95 us
  other arithmetic: 81.7 us -> 65.8 us
    reduce_scatter x0 -> x5, waiting for transfers between devices: none -> 223 us  [the longest x4 173 us: summed_columns(): lax.psum_scatter(value.astype(jnp.bfloat16), 'tp', scatter_dimension=1, t...]
    all_to_all x5 -> x0, waiting for transfers between devices: 218 us -> none  [the longest x1 69.9 us: local(): lax.all_to_all(unfold_rows(expert_part).astype(jnp.bfloat16), ('shard', '...]
    all_gather x0 -> x6, waiting for transfers between devices: none -> 211 us  [the longest x2 82.3 us: rows_for_expert(): return lax.all_gather(everyone[ranking], 'tp', axis=1, tiled=True)]
    psum x2 -> x1, waiting for transfers between devices: 228 us -> 87.3 us  [local(): lax.psum(normed_part.astype(jnp.bfloat16), 'tp').astype(jnp.float32)]
    all_to_all x1, blocking collectives: 76.9 us -> 24.3 us  [local(): lax.all_to_all(sent_grad, 'ctx', split_axis=0, concat_axis=0, tiled=True)]
    unnamed x13 -> x23, waiting for transfers between devices: 49 us -> 4.55 us
    scatter x4 -> x0, local copies, waits for them, and re-layouts: 43.7 us -> none  [the longest x2 28.8 us: unfold_rows(): buffer.at[ranking].set(slot_rows)]
    gather x5 -> x2, local copies, waits for them, and re-layouts: 48.8 us -> 13.4 us  [rows_for_expert(): return lax.all_gather(everyone[ranking], 'tp', axis=1, tiled=True)]
  transfers between devices with their start and end apart: 17 -> 22, of which waited for: 11 -> 17; matrix products, arithmetic and copies ran while one was open for 17% -> 18% of each run, Pallas kernels for 3% -> 3%
where the time goes in v2:
time: 1100 us
  waiting for transfers between devices  654 us (59%)
  blocking collectives  126 us (11%)
  matrix products  103 us (9%)
  other arithmetic  65.8 us (6%)
  local copies, waits for them, and re-layouts  65.4 us (6%)
  Pallas kernels  54.6 us (5%)
  between operations  15.8 us (1%)
    reduce_scatter x4, waiting for transfers between devices, summed_columns(): lax.psum_scatter(value.astype(jnp.bfloat16), 'tp', scatter_dimension=1, t...  173 us
    psum x1, waiting for transfers between devices, local(): lax.psum(normed_part.astype(jnp.bfloat16), 'tp').astype(jnp.float32)  87.3 us
    psum x1, waiting for transfers between devices, local(): lax.psum(branch_part.astype(jnp.bfloat16), 'tp').astype(jnp.float32)  87.1 us
    all_gather x2, waiting for transfers between devices, rows_for_expert(): return lax.all_gather(everyone[ranking], 'tp', axis=1, tiled=True)  82.3 us
    all_gather x2, waiting for transfers between devices, rows_for_expert(): everyone = lax.all_gather(columns(value), group, axis=0, tiled=True)  59.5 us
    reduce_scatter x1, waiting for transfers between devices, local(): lax.psum_scatter(placed, group, scatter_dimension=0, tiled=True)  49.8 us
    all_gather x1, waiting for transfers between devices, local(): layer_out = lax.all_gather(out_cols, 'tp', axis=1, tiled=True)[None]  40.8 us
    unnamed x84, local copies, waits for them, and re-layouts  33.9 us
  transfers between devices with their start and end apart: 22, of which 17 were waited for; matrix products, arithmetic and copies ran while one was open for 18% of the time, Pallas kernels for 3%

profile of v2, /device:TPU:0, one launch (start us, length us, event | category | flops | bytes accessed | tf_op | source)
XLA Modules:
  0.0 1095.1 jit_solution(2523676303320713422)
XLA Ops:
  11.9 25.3 %all-gather.4 = f32[8,1,1536]{2,1,0:T(1,128)S(1)} all-gather(f32[1,1,1536]{2,1,0:T(1,128)S(1)} %reshape.221), channel_id=2, replica_groups=mesh['shard'=2,'ctx'=4,'tp'=4] {'shard','ctx'}, dimensions={0}, use_global_device_ids=true | all-gather | bytes 55296 | tf_op jit(solution)/shard_map/all_gather | solution.py:233
  45.8 22.5 %all_to_all.20.qkv_ref = bf16[4,3,64,1024]{3,2,1,0:T(8,128)(2,1)S(1)} all-to-all(bf16[4,3,64,1024]{3,2,1,0:T(8,128)(2,1)S(1)} %bitcast.237), channel_id=1, replica_groups=mesh['shard'=2,'ctx'=4,'tp'=4] {'ctx'}, dimensions={0} | all-to-all | bytes 3145728 | tf_op jit(solution)/shard_map/all_to_all | solution.py:278
  68.3 23.6 %flash_forward.1 = (bf16[4,64,1024]{2,1,0:T(8,128)(2,1)}, f32[4,64,1024]{2,1,0:T(8,128)S(1)}, f32[4,1,1024]{2,1,0:T(1,128)S(1)}) custom-call(bf16[4,3,64,1024]{3,2,1,0:T(8,128)(2,1)S(1)} %all_to_all.20.qkv_ref), custom_call_target="tpu_custom_call" | custom-call | flops 8589934592 | bytes 5242880 | tf_op jit(solution)/shard_map/flash_forward/pallas_call | solution.py:101
  96.1 26.6 %all_gather.40 = bf16[256,1024]{1,0:T(8,128)(2,1)} all-gather(bf16[256,128]{1,0:T(8,128)(2,1)S(1)} %copy-done.17), channel_id=1, replica_groups=mesh['shard'=2,'ctx'=4,'tp'=4] {'shard','ctx'}, dimensions={1}, use_global_device_ids=true | all-gather | bytes 589824 | tf_op jit(solution)/shard_map/all_gather | solution.py:266
  126.1 87.1 %all-reduce.4.cloned.1.call-done = bf16[1024,1024]{1,0:T(8,128)(2,1)} async-done(((bf16[1024,1024]{1,0:T(8,128)(2,1)}), bf16[1024,1024]{1,0:T(8,128)(2,1)}) %all-reduce.4.cloned.1.call-update) | async-done | bytes 2097168 | tf_op jit(solution)/shard_map/psum | solution.py:286
  223.0 6.2 sort.15
  229.2 27.3 %all-gather.21.cloned.1.call-done = bf16[8192,256]{1,0:T(8,128)(2,1)} async-done(((bf16[1024,256]{1,0:T(8,128)(2,1)}), bf16[8192,256]{1,0:T(8,128)(2,1)}) %all-gather.21.cloned.1.call-update) | async-done | bytes 4194320 | tf_op jit(solution)/shard_map/all_gather | solution.py:259
  256.5 6.7 gather_fusion
  263.3 32.2 %all-gather.29.cloned.1.call-done = bf16[1,8192,256]{2,1,0:T(8,128)(2,1)} async-done(((bf16[1,1024,256]{2,1,0:T(8,128)(2,1)}), bf16[1,8192,256]{2,1,0:T(8,128)(2,1)}) %all-gather.29.cloned.1.call-update) | async-done | bytes 4194320 | tf_op jit(solution)/shard_map/all_gather | solution.py:259
  295.5 6.7 gather_fusion.1
  302.2 45.8 %all-gather.27.cloned.1.call-done = bf16[1152,1024]{1,0:T(8,128)(2,1)} async-done(((bf16[1152,256]{1,0:T(8,128)(2,1)}), bf16[1152,1024]{1,0:T(8,128)(2,1)}) %all-gather.27.cloned.1.call-update) | async-done | bytes 2359312 | tf_op jit(solution)/shard_map/all_gather | solution.py:260
  362.3 36.5 %all-gather.31.cloned.1.call-done = bf16[1152,1024]{1,0:T(8,128)(2,1)} async-done(((bf16[1152,256]{1,0:T(8,128)(2,1)}), bf16[1152,1024]{1,0:T(8,128)(2,1)}) %all-gather.31.cloned.1.call-update) | async-done | bytes 2359312 | tf_op jit(solution)/shard_map/all_gather | solution.py:260
  398.8 7.7 fusion.15
  413.2 34.4 %reduce-scatter.18.cloned.1.call-done = bf16[1152,256]{1,0:T(8,128)(2,1)} async-done(((bf16[1152,1024]{1,0:T(8,128)(2,1)}), bf16[1152,256]{1,0:T(8,128)(2,1)}) %reduce-scatter.18.cloned.1.call-update) | async-done | bytes 589840 | tf_op jit(solution)/shard_map/reduce_scatter | solution.py:310
  447.6 50.0 %reduce-scatter.20.cloned.1.call-done = bf16[1152,256]{1,0:T(8,128)(2,1)} async-done(((bf16[1152,1024]{1,0:T(8,128)(2,1)}), bf16[1152,256]{1,0:T(8,128)(2,1)}) %reduce-scatter.20.cloned.1.call-update) | async-done | bytes 589840 | tf_op jit(solution)/shard_map/reduce_scatter | solution.py:310
  497.6 13.5 %scatter_custom_fusion = bf16[8192,512]{1,0:T(8,128)(2,1)} fusion(s32[1152]{0:T(1024)S(1)} %get-tuple-element.81, bf16[]{:T(256)} %constant.19.clone.1, bf16[1152,256]{1,0:T(8,128)(2,1)} %reduce-scatter.20.cloned.1.call-done, bf16[]{:T(256)} %constant.85, bf16[1152,256]{1,0:T(8,128)(2,1)} %reduce-scatter.18.cloned.1.call-done), kind=kCustom, calls=%fused_computation.54 | custom fusion | flops 2359296 | bytes 9568260 | tf_op jit(solution)/shard_map/scatter | solution.py:337
  513.4 13.2 %all-gather.17.cloned.1.call-done = bf16[1024,1024]{1,0:T(8,128)(2,1)} async-done(((bf16[128,1024]{1,0:T(8,128)(2,1)}), bf16[1024,1024]{1,0:T(8,128)(2,1)}) %all-gather.17.cloned.1.call-update) | async-done | bytes 2097168 | tf_op jit(solution)/shard_map/all_gather | solution.py:267
  532.6 23.9 %all-gather.19.cloned.1.call-done = bf16[1024,1024]{1,0:T(8,128)(2,1)} async-done(((bf16[1024,128]{1,0:T(8,128)(2,1)}), bf16[1024,1024]{1,0:T(8,128)(2,1)}) %all-gather.19.cloned.1.call-update) | async-done | bytes 2097168 | tf_op jit(solution)/shard_map/all_gather | solution.py:268
  556.5 7.9 fusion.30
  569.7 8.0 convolution_convert_fusion.5
  581.7 49.8 %reduce-scatter.22.cloned.1.call-done = bf16[1024,512]{1,0:T(8,128)(2,1)} async-done(((bf16[8192,512]{1,0:T(8,128)(2,1)}), bf16[1024,512]{1,0:T(8,128)(2,1)}) %reduce-scatter.22.cloned.1.call-update) | async-done | bytes 1048592 | tf_op jit(solution)/shard_map/reduce_scatter | solution.py:339
  634.4 42.9 %reduce-scatter.24.cloned.1.call-done = bf16[1024,256]{1,0:T(8,128)(2,1)} async-done(((bf16[1024,1024]{1,0:T(8,128)(2,1)}), bf16[1024,256]{1,0:T(8,128)(2,1)}) %reduce-scatter.24.cloned.1.call-update) | async-done | bytes 524304 | tf_op jit(solution)/shard_map/reduce_scatter | solution.py:310
  677.3 45.7 %reduce-scatter.16.cloned.1.call-done = bf16[1024,256]{1,0:T(8,128)(2,1)} async-done(((bf16[1024,1024]{1,0:T(8,128)(2,1)}), bf16[1024,256]{1,0:T(8,128)(2,1)}) %reduce-scatter.16.cloned.1.call-update) | async-done | bytes 524304 | tf_op jit(solution)/shard_map/reduce_scatter | solution.py:310
  728.8 7.4 convolution_convert_fusion.2
  745.6 28.0 %all-gather.25.cloned.1.call-done = bf16[4,1032,256]{2,1,0:T(8,128)(2,1)} async-done(((bf16[1,1032,256]{2,1,0:T(8,128)(2,1)}), bf16[4,1032,256]{2,1,0:T(8,128)(2,1)}) %all-gather.25.cloned.1.call-update) | async-done | bytes 2113552 | tf_op jit(solution)/shard_map/all_gather | solution.py:349
  791.2 6.4 multiply_reduce_fusion
  821.6 31.1 %flash_backward.1 = bf16[4,3,64,1024]{3,2,1,0:T(8,128)(2,1)S(1)} custom-call(bf16[4,3,64,1024]{3,2,1,0:T(8,128)(2,1)S(1)} %copy-done.3, bf16[4,64,1024]{2,1,0:T(8,128)(2,1)S(1)} %all-to-all-done.2.grad_ref, f32[4,64,1024]{2,1,0:T(8,128)S(1)} %get-tuple-element.19.wide_ref, f32[4,1,1024]{2,1,0:T(1,128)S(1)} %get-tuple-element.20.lse_ref), custom_call_target="tpu_custom_call" | custom-call | flops 21474836480 | bytes 8388608 | tf_op jit(solution)/shard_map/flash_backward/pallas_call | solution.py:180
  852.7 24.3 %all_to_all.21 = bf16[4,3,64,1024]{3,2,1,0:T(8,128)(2,1)S(1)} all-to-all(bf16[4,3,64,1024]{3,2,1,0:T(8,128)(2,1)S(1)} %flash_backward.1), channel_id=1, replica_groups=mesh['shard'=2,'ctx'=4,'tp'=4] {'ctx'}, dimensions={0} | all-to-all | bytes 3145728 | tf_op jit(solution)/shard_map/all_to_all | solution.py:373
  886.1 7.5 convolution_bitcast_fusion.1
  914.0 40.8 %all-gather.23.cloned.1.call-done = bf16[1024,1024]{1,0:T(8,128)(2,1)} async-done(((bf16[1024,256]{1,0:T(8,128)(2,1)}), bf16[1024,1024]{1,0:T(8,128)(2,1)}) %all-gather.23.cloned.1.call-update) | async-done | bytes 2097168 | tf_op jit(solution)/shard_map/all_gather | solution.py:343
  954.8 87.3 %all-reduce.6.cloned.1.call-done = bf16[1024,1024]{1,0:T(8,128)(2,1)} async-done(((bf16[1024,1024]{1,0:T(8,128)(2,1)}), bf16[1024,1024]{1,0:T(8,128)(2,1)}) %all-reduce.6.cloned.1.call-update) | async-done | bytes 2097168 | tf_op jit(solution)/shard_map/psum | solution.py:379
  1045.6 26.9 %all-reduce = f32[8,4,128]{2,1,0:T(4,128)S(1)} all-reduce(f32[8,4,128]{2,1,0:T(4,128)S(1)} %maximum_bitcast_fusion), channel_id=11, replica_groups=mesh['shard'=2,'ctx'=4,'tp'=4] {'shard','ctx'}, use_global_device_ids=true, to_apply=%region_27.28.clone | all-reduce | flops 4096 | bytes 32768
  (211 shorter events, 176.1 us)
Async XLA Ops:
  7.2 347.9 %copy-start = (bf16[1,1024,1024]{2,1,0:T(8,128)(2,1)S(1)}, bf16[1,1024,1024]{2,1,0:T(8,128)(2,1)}, u32[]{:S(2)}) copy-start(bf16[1,1024,1024]{2,1,0:T(8,128)(2,1)} %param.26) | copy-start | bytes 6291460
  7.2 34.4 %all-gather.15.cloned.1.call-start = ((), (), s32[]{:S(2)}) async-start(), calls=%async_computation.13 | async-start | bytes 1769472 | tf_op jit(solution)/shard_map/all_gather | solution.py:263
  68.3 23.6 %copy-start.2 = (bf16[4,3,64,1024]{3,2,1,0:T(8,128)(2,1)}, bf16[4,3,64,1024]{3,2,1,0:T(8,128)(2,1)S(1)}, u32[]{:S(2)}) copy-start(bf16[4,3,64,1024]{3,2,1,0:T(8,128)(2,1)S(1)} %all_to_all.20.qkv_ref) | copy-start | bytes 4718596
  68.3 27.8 %copy-start.17 = (bf16[256,128]{1,0:T(8,128)(2,1)S(1)}, bf16[256,128]{1,0:T(8,128)(2,1)}, u32[]{:S(2)}) copy-start(bf16[256,128]{1,0:T(8,128)(2,1)} %param.20) | copy-start | bytes 196612
  91.9 30.8 %all-to-all-start.1 = ((bf16[4,64,1024]{2,1,0:T(8,128)(2,1)}), bf16[4,64,1024]{2,1,0:T(8,128)(2,1)}, u32[]{:S(2)}, u32[]{:S(2)}) async-start(bf16[4,64,1024]{2,1,0:T(8,128)(2,1)} %get-tuple-element.16), calls=%async_computation.1 | async-start | bytes 1048576 | tf_op jit(solution)/shard_map/all_to_all | solution.py:280
  96.1 117.2 %all-reduce.4.cloned.1.call-start = ((), (), s32[]{:S(2)}) async-start(), calls=%async_computation.14 | async-start | bytes 4194304 | tf_op jit(solution)/shard_map/psum | solution.py:286
  126.0 130.5 %all-gather.21.cloned.1.call-start = ((), (), s32[]{:S(2)}) async-start(), calls=%async_computation.18 | async-start | bytes 4718592 | tf_op jit(solution)/shard_map/all_gather | solution.py:259
  220.8 74.7 %all-gather.29.cloned.1.call-start = ((), (), s32[]{:S(2)}) async-start(), calls=%async_computation.28 | async-start | bytes 4718592 | tf_op jit(solution)/shard_map/all_gather | solution.py:259
  222.7 125.3 %all-gather.27.cloned.1.call-start = ((), (), s32[]{:S(2)}) async-start(), calls=%async_computation.27 | async-start | bytes 2949120 | tf_op jit(solution)/shard_map/all_gather | solution.py:260
  263.3 135.5 %all-gather.31.cloned.1.call-start = ((), (), s32[]{:S(2)}) async-start(), calls=%async_computation.29 | async-start | bytes 2949120 | tf_op jit(solution)/shard_map/all_gather | solution.py:260
  302.2 145.4 %reduce-scatter.18.cloned.1.call-start = ((), (), s32[]{:S(2)}) async-start(), calls=%async_computation.19 | async-start | bytes 2949120 | tf_op jit(solution)/shard_map/reduce_scatter | solution.py:310
  359.3 138.2 %reduce-scatter.20.cloned.1.call-start = ((), (), s32[]{:S(2)}) async-start(), calls=%async_computation.20 | async-start | bytes 2949120 | tf_op jit(solution)/shard_map/reduce_scatter | solution.py:310
  398.8 9.1 copy-start.25
  411.8 114.8 %all-gather.17.cloned.1.call-start = ((), (), s32[]{:S(2)}) async-start(), calls=%async_computation.15 | async-start | bytes 2359296 | tf_op jit(solution)/shard_map/all_gather | solution.py:267
  412.6 144.0 %all-gather.19.cloned.1.call-start = ((), (), s32[]{:S(2)}) async-start(), calls=%async_computation.16 | async-start | bytes 2359296 | tf_op jit(solution)/shard_map/all_gather | solution.py:268
  413.1 218.4 %reduce-scatter.22.cloned.1.call-start = ((), (), s32[]{:S(2)}) async-start(), calls=%async_computation.21 | async-start | bytes 9437184 | tf_op jit(solution)/shard_map/reduce_scatter | solution.py:339
  511.1 166.2 %reduce-scatter.24.cloned.1.call-start = ((), (), s32[]{:S(2)}) async-start(), calls=%async_computation.23 | async-start | bytes 2621440 | tf_op jit(solution)/shard_map/reduce_scatter | solution.py:310
  556.5 9.3 copy-start.26
  569.6 153.4 %reduce-scatter.16.cloned.1.call-start = ((), (), s32[]{:S(2)}) async-start(), calls=%async_computation.17 | async-start | bytes 2621440 | tf_op jit(solution)/shard_map/reduce_scatter | solution.py:310
  577.7 195.9 %all-gather.25.cloned.1.call-start = ((), (), s32[]{:S(2)}) async-start(), calls=%async_computation.24 | async-start | bytes 2641920 | tf_op jit(solution)/shard_map/all_gather | solution.py:349
  728.3 154.0 %reduce-scatter.32.cloned.1.call-start = ((), (), s32[]{:S(2)}) async-start(), calls=%async_computation.32 | async-start | bytes 2359296
  740.2 144.1 %reduce-scatter.26.cloned.1.call-start = ((), (), s32[]{:S(2)}) async-start(), calls=%async_computation.26 | async-start | bytes 2359296 | tf_op jit(solution)/shard_map/reduce_scatter | solution.py:383
  745.6 166.8 %reduce-scatter.30.cloned.1.call-start = ((), (), s32[]{:S(2)}) async-start(), calls=%async_computation.31 | async-start | bytes 589824
  806.1 15.5 %copy-start.3 = (bf16[4,3,64,1024]{3,2,1,0:T(8,128)(2,1)S(1)}, bf16[4,3,64,1024]{3,2,1,0:T(8,128)(2,1)}, u32[]{:S(2)}) copy-start(bf16[4,3,64,1024]{3,2,1,0:T(8,128)(2,1)} %copy-done.2) | copy-start | bytes 4718596
  810.0 11.6 %all-to-all-start.2 = ((bf16[4,64,1024]{2,1,0:T(8,128)(2,1)}), bf16[4,64,1024]{2,1,0:T(8,128)(2,1)S(1)}, u32[]{:S(2)}, u32[]{:S(2)}) async-start(bf16[4,64,1024]{2,1,0:T(8,128)(2,1)} %bitcast.240), calls=%async_computation.7 | async-start | bytes 1048576 | tf_op jit(solution)/shard_map/all_to_all | solution.py:369
  813.7 141.1 %all-gather.23.cloned.1.call-start = ((), (), s32[]{:S(2)}) async-start(), calls=%async_computation.22 | async-start | bytes 2621440 | tf_op jit(solution)/shard_map/all_gather | solution.py:343
  816.7 225.4 %all-reduce.6.cloned.1.call-start = ((), (), s32[]{:S(2)}) async-start(), calls=%async_computation.25 | async-start | bytes 4194304 | tf_op jit(solution)/shard_map/psum | solution.py:379
  852.7 25.6 %copy-start.27 = (bf16[3,1024,256]{1,2,0:T(8,128)(2,1)S(1)}, bf16[3,1024,256]{1,2,0:T(8,128)(2,1)}, u32[]{:S(2)}) copy-start(bf16[3,1024,256]{1,2,0:T(8,128)(2,1)} %all-gather.15.cloned.1.call-done) | copy-start | bytes 4718596
  878.3 15.3 %slice-start = ((s8[4718592]{0:T(1024)(128)(4,1)}), s8[524288]{0:T(1024)(128)(4,1)S(1)}, s32[]{:S(2)}) async-start(s8[4718592]{0:T(1024)(128)(4,1)} %bitcast.263), calls=%async_computation.33 | async-start | bytes 1048576
  881.5 201.3 %reduce-scatter.28.cloned.1.call-start = ((), (), s32[]{:S(2)}) async-start(), calls=%async_computation.30 | async-start | bytes 1769472
  886.1 7.5 slice-start.1
  1074.2 13.8 %copy-start.1 = (bf16[1,1024,1024]{2,1,0:T(8,128)(2,1)S(1)}, bf16[1,1024,1024]{2,1,0:T(8,128)(2,1)}, u32[]{:S(2)}) copy-start(bf16[1,1024,1024]{2,1,0:T(8,128)(2,1)} %param.26) | copy-start | bytes 6291460
  (24 other events, 100.6 us)
Sparse Core Ops, SparseCore 0:
  10.5 28.6 all-gather.14
  126.2 87.0 all-reduce.3
  220.9 35.6 all-gather.20
  258.9 36.5 all-gather.28
  297.5 50.5 all-gather.26
  350.0 48.7 all-gather.30
  401.7 45.8 reduce-scatter.17
  450.4 47.0 reduce-scatter.19
  499.5 27.1 all-gather.16
  528.4 28.0 all-gather.18
  560.0 71.4 reduce-scatter.21
  633.7 43.6 reduce-scatter.23
  680.2 42.8 reduce-scatter.15
  728.4 45.1 all-gather.24
  776.7 39.9 reduce-scatter.31
  819.8 50.0 reduce-scatter.25
  872.8 34.2 reduce-scatter.29
  908.5 46.2 all-gather.22
  957.7 84.2 all-reduce.5
  1045.2 37.5 reduce-scatter.27

commit v3 on v2

--- a/solution.py
+++ b/solution.py
@@ -108,7 +108,7 @@
         ),
         scratch_shapes=[pltpu.VMEM((chunks * chunk, width), jnp.bfloat16)],
         cost_estimate=pl.CostEstimate(
-            flops=2 * (chunks * chunk) ** 2 * width * 4, bytes_accessed=5 << 20, transcendentals=0
+            flops=24 * 10 ** 9, bytes_accessed=5 << 20, transcendentals=0
         ),
         compiler_params=pltpu.CompilerParams(vmem_limit_bytes=40 << 20),
     )(qkv)
@@ -191,7 +191,7 @@
             pltpu.VMEM((chunks, width, chunk), jnp.float32),
         ],
         cost_estimate=pl.CostEstimate(
-            flops=2 * full ** 2 * width * 10, bytes_accessed=8 << 20, transcendentals=0
+            flops=32 * 10 ** 9, bytes_accessed=8 << 20, transcendentals=0
         ),
         compiler_params=pltpu.CompilerParams(vmem_limit_bytes=48 << 20),
     )(qkv, grad, wide, lse)
@@ -283,7 +283,10 @@
     branch_part = jnp.einsum(
         "ft,fd->td", attended_low, proj_full, preferred_element_type=jnp.float32
     )
-    branch = lax.psum(branch_part.astype(jnp.bfloat16), "tp").astype(jnp.float32)
+    branch_low, up_full, down_full, grad_rows = lax.optimization_barrier(
+        (branch_part.astype(jnp.bfloat16), up_full, down_full, grad_rows)
+    )
+    branch = lax.psum(branch_low, "tp").astype(jnp.float32)
     middle = inputs + branch
     normed2, unit_two, inverse_two = norm_forward(middle, gain_two)
     normed2_low = normed2.astype(jnp.bfloat16)
@@ -293,19 +296,6 @@
     upper_pre = jnp.dot(normed2_low, up_full, preferred_element_type=jnp.float32)
     hidden_low = gelu_tanh(upper_pre).astype(jnp.bfloat16)
     dense_part = jnp.dot(hidden_low, down_full, preferred_element_type=jnp.float32)
-    own_up = expert_up[0]
-    own_down = expert_down[0]
-    expert_in = rows_for_expert(normed2_low)
-    expert_mixing = jax.nn.softmax(
-        jnp.dot(expert_in, mix_full, preferred_element_type=jnp.float32), axis=-1
-    )
-    grad_in = (expert_mixing[:, 1:2] * grad_rows.astype(jnp.float32) * taken_mask).astype(
-        jnp.bfloat16
-    )
-    expert_pre = jnp.dot(expert_in, own_up, preferred_element_type=jnp.float32)
-    expert_hidden = gelu_tanh(expert_pre).astype(jnp.bfloat16)
-    expert_part = jnp.dot(expert_hidden, own_down, preferred_element_type=jnp.float32)
-
     def summed_columns(value):
         return lax.psum_scatter(
             value.astype(jnp.bfloat16), "tp", scatter_dimension=1, tiled=True
@@ -313,14 +303,37 @@
 
     out_grad = cotangent[0].astype(jnp.float32) * live_rows
     dense_grad = (mixing[:, 0:1] * out_grad).astype(jnp.bfloat16)
-    dense_cols = summed_columns(dense_part).astype(jnp.float32)
-    expert_cols = summed_columns(expert_part)
     down_grad = jnp.einsum("tf,td->fd", hidden_low, dense_grad, preferred_element_type=jnp.float32)
     hidden_grad = jnp.einsum("td,fd->tf", dense_grad, down_full, preferred_element_type=jnp.float32)
     _, gelu_pull = jax.vjp(gelu_tanh, upper_pre)
     upper_grad = gelu_pull(hidden_grad)[0].astype(jnp.bfloat16)
     up_grad = jnp.einsum("td,tf->df", normed2_low, upper_grad, preferred_element_type=jnp.float32)
     normed2_part = jnp.einsum("tf,df->td", upper_grad, up_full, preferred_element_type=jnp.float32)
+    own_up = expert_up[0]
+    own_down = expert_down[0]
+    expert_in, dense_low, normed2_part = lax.optimization_barrier(
+        (
+            rows_for_expert(normed2_low),
+            dense_part.astype(jnp.bfloat16),
+            normed2_part.astype(jnp.bfloat16),
+        )
+    )
+    dense_cols = summed_columns(dense_low)
+    expert_mixing = jax.nn.softmax(
+        jnp.dot(expert_in, mix_full, preferred_element_type=jnp.float32), axis=-1
+    )
+    grad_in = (expert_mixing[:, 1:2] * grad_rows.astype(jnp.float32) * taken_mask).astype(
+        jnp.bfloat16
+    )
+    expert_pre = jnp.dot(expert_in, own_up, preferred_element_type=jnp.float32)
+    expert_hidden = gelu_tanh(expert_pre).astype(jnp.bfloat16)
+    expert_part = jnp.dot(expert_hidden, own_down, preferred_element_type=jnp.float32)
+
+    expert_low, dense_cols = lax.optimization_barrier(
+        (expert_part.astype(jnp.bfloat16), dense_cols)
+    )
+    dense_cols = dense_cols.astype(jnp.float32)
+    expert_cols = summed_columns(expert_low)
     own_down_grad = jnp.einsum(
         "cf,cd->fd", expert_hidden, grad_in, preferred_element_type=jnp.float32
     )
@@ -369,7 +382,15 @@
     heads_grad = lax.all_to_all(
         attended_grad.reshape(ctx_size, HD, seq_dev), "ctx", split_axis=0, concat_axis=0, tiled=True
     )
+    def shared(value, axis):
+        return lax.psum_scatter(
+            value.astype(jnp.bfloat16), group, scatter_dimension=axis, tiled=True
+        ).astype(jnp.float32)
+
     sent_grad = flash_backward(qkv, heads_grad, heads_wide, log_total)
+    sent_grad, layer_out, up_share, down_share, proj_share = lax.optimization_barrier(
+        (sent_grad, layer_out, shared(up_grad, 0), shared(down_grad, 1), shared(proj_grad, 1))
+    )
     qkv_grad = lax.all_to_all(sent_grad, "ctx", split_axis=0, concat_axis=0, tiled=True)
     qkv_grad = jnp.swapaxes(qkv_grad, 0, 1).reshape(3, ctx_size * HD, seq_dev)
     qkv_grad_full = jnp.einsum(
@@ -377,24 +398,23 @@
     )
     normed_part = jnp.einsum("cft,cdf->td", qkv_grad, qkv_full, preferred_element_type=jnp.float32)
     normed_grad = lax.psum(normed_part.astype(jnp.bfloat16), "tp").astype(jnp.float32)
-    input_norm_grad, gain_one_grad = norm_backward(normed_grad, gain_one, unit_one, inverse_one)
+    input_norm_grad, _ = norm_backward(normed_grad, gain_one, unit_one, inverse_one)
     tokens_grad = (middle_grad + input_norm_grad).astype(jnp.bfloat16)[None]
-    def shared(value, axis):
-        return lax.psum_scatter(
-            value.astype(jnp.bfloat16), group, scatter_dimension=axis, tiled=True
-        ).astype(jnp.float32)
-
-    small_grad = jnp.concatenate([gain_one_grad[None], gain_two_grad[None], mix_grad.T], axis=0)
+    gain_one_grad = jnp.sum(qkv_grad_full * qkv_full.astype(jnp.float32), axis=(0, 2)) / gain_one
+    replicas = 1.0 / lax.axis_size("tp")
+    small_grad = jnp.concatenate(
+        [gain_one_grad[None], replicas * gain_two_grad[None], replicas * mix_grad.T], axis=0
+    )
     small_grad = jnp.swapaxes(small_grad.reshape(4, members, -1), 0, 1)
-    small_grad = lax.psum_scatter(small_grad, group, scatter_dimension=0, tiled=True)[0]
+    small_grad = lax.psum(small_grad, ("shard", "ctx", "tp"))[lax.axis_index(group)]
     shares = (
         small_grad[0],
         jnp.swapaxes(shared(qkv_grad_full, 1), 0, 1),
-        shared(proj_grad, 1),
+        proj_share,
         small_grad[1],
         small_grad[2:].T,
-        shared(up_grad, 0),
-        shared(down_grad, 1),
+        up_share,
+        down_share,
     )
     return (
         layer_out,

time: 1100 us -> 1080 us (0.982)
  blocking collectives: 126 us -> 98.7 us
    psum x1, waiting for transfers between devices: 87.3 us -> 16.2 us  [local(): lax.psum(normed_part.astype(jnp.bfloat16), 'tp').astype(jnp.float32)]
    unnamed x23, waiting for transfers between devices: 4.55 us -> 59.3 us
    all_to_all x2 -> x0, blocking collectives: 46.8 us -> none  [the longest x1 24.3 us: local(): lax.all_to_all(sent_grad, 'ctx', split_axis=0, concat_axis=0, tiled=True)]
    reduce_scatter x1, waiting for transfers between devices: 0.01 us -> 42.9 us  [shared(): lax.psum_scatter(value.astype(jnp.bfloat16), group, scatter_dimension=axi...]
    psum x0 -> x1, blocking collectives: none -> 40.2 us  [local(): lax.psum(small_grad, ('shard', 'ctx', 'tp'))[lax.axis_index(group)]]
    unnamed x1 -> x0, blocking collectives: 26.9 us -> none
    all_gather x1, waiting for transfers between devices: 23.9 us -> 0.01 us  [local(): down_full = lax.all_gather(down_weight, group, axis=1, tiled=True)]
    all_to_all x0 -> x2, waiting for transfers between devices: none -> 19.3 us  [the longest x1 19.3 us: local(): lax.all_to_all(sent_grad, 'ctx', split_axis=0, concat_axis=0, tiled=True)]
  transfers between devices with their start and end apart: 22 -> 24, of which waited for: 17 -> 18; matrix products, arithmetic and copies ran while one was open for 18% -> 15% of each run, Pallas kernels for 3% -> 6%
where the time goes in v3:
time: 1080 us; the launch traced here: 1070 us
  waiting for transfers between devices  660 us (61%)
  matrix products  100 us (9%)
  blocking collectives  98.7 us (9%)
  Pallas kernels  59 us (5%)
  other arithmetic  58.7 us (5%)
  local copies, waits for them, and re-layouts  55.5 us (5%)
  starting transfers between devices  18.1 us (2%)
  between operations  15.9 us (1%)
    reduce_scatter x4, waiting for transfers between devices, summed_columns(): lax.psum_scatter(value.astype(jnp.bfloat16), 'tp', scatter_dimension=1, t...  159 us
    psum x1, waiting for transfers between devices, local(): branch = lax.psum(branch_low, 'tp').astype(jnp.float32)  86.8 us
    all_gather x2, waiting for transfers between devices, rows_for_expert(): return lax.all_gather(everyone[ranking], 'tp', axis=1, tiled=True)  74.3 us
    reduce_scatter x1, waiting for transfers between devices, local(): lax.psum_scatter(placed, group, scatter_dimension=0, tiled=True)  67.2 us
    all_gather x2, waiting for transfers between devices, rows_for_expert(): everyone = lax.all_gather(columns(value), group, axis=0, tiled=True)  60.1 us
    unnamed x23, waiting for transfers between devices  59.3 us
    all_gather x1, waiting for transfers between devices, local(): layer_out = lax.all_gather(out_cols, 'tp', axis=1, tiled=True)[None]  46.1 us
    reduce_scatter x1, waiting for transfers between devices, shared(): lax.psum_scatter(value.astype(jnp.bfloat16), group, scatter_dimension=axi...  42.9 us
  transfers between devices with their start and end apart: 24, of which 18 were waited for; matrix products, arithmetic and copies ran while one was open for 15% of the time, Pallas kernels for 6%

profile of v3, /device:TPU:0, one launch (start us, length us, event | category | flops | bytes accessed | tf_op | source)
XLA Modules:
  0.0 1066.6 jit_solution(7268584884796491351)
XLA Ops:
  15.2 25.3 %all-gather.4 = f32[8,1,1536]{2,1,0:T(1,128)S(1)} all-gather(f32[1,1,1536]{2,1,0:T(1,128)S(1)} %reshape.237), channel_id=2, replica_groups=mesh['shard'=2,'ctx'=4,'tp'=4] {'shard','ctx'}, dimensions={0}, use_global_device_ids=true | all-gather | bytes 55296 | tf_op jit(solution)/shard_map/all_gather | solution.py:233
  54.6 6.2 sort.15
  60.8 26.7 %all-gather.27.cloned.1.call-done = bf16[1,8192,256]{2,1,0:T(8,128)(2,1)} async-done(((bf16[1,1024,256]{2,1,0:T(8,128)(2,1)}), bf16[1,8192,256]{2,1,0:T(8,128)(2,1)}) %all-gather.27.cloned.1.call-update) | async-done | bytes 4194320 | tf_op jit(solution)/shard_map/all_gather | solution.py:259
  87.5 6.7 gather_fusion
  94.2 25.3 %flash_forward.1 = (bf16[4,64,1024]{2,1,0:T(8,128)(2,1)}, f32[4,64,1024]{2,1,0:T(8,128)S(1)}, f32[4,1,1024]{2,1,0:T(1,128)S(1)}) custom-call(bf16[4,3,64,1024]{3,2,1,0:T(8,128)(2,1)} %all-to-all-done.qkv_ref), custom_call_target="tpu_custom_call" | custom-call | flops 24000000000 | bytes 5242880 | tf_op jit(solution)/shard_map/flash_forward/pallas_call | solution.py:101
  123.7 33.2 %all_gather.40 = bf16[256,1024]{1,0:T(8,128)(2,1)} all-gather(bf16[256,128]{1,0:T(8,128)(2,1)S(1)} %copy-done.22), channel_id=1, replica_groups=mesh['shard'=2,'ctx'=4,'tp'=4] {'shard','ctx'}, dimensions={1}, use_global_device_ids=true | all-gather | bytes 589824 | tf_op jit(solution)/shard_map/all_gather | solution.py:266
  160.2 45.8 %all-gather.29.cloned.1.call-done = bf16[1152,1024]{1,0:T(8,128)(2,1)} async-done(((bf16[1152,256]{1,0:T(8,128)(2,1)}), bf16[1152,1024]{1,0:T(8,128)(2,1)}) %all-gather.29.cloned.1.call-update) | async-done | bytes 2359312 | tf_op jit(solution)/shard_map/all_gather | solution.py:260
  206.3 86.8 %all-reduce.3.cloned.1.call-done = bf16[1024,1024]{1,0:T(8,128)(2,1)} async-done(((bf16[1024,1024]{1,0:T(8,128)(2,1)}), bf16[1024,1024]{1,0:T(8,128)(2,1)}) %all-reduce.3.cloned.1.call-update) | async-done | bytes 2097168 | tf_op jit(solution)/shard_map/psum | solution.py:289
  304.9 33.4 %all-gather.21.cloned.1.call-done = bf16[8192,256]{1,0:T(8,128)(2,1)} async-done(((bf16[1024,256]{1,0:T(8,128)(2,1)}), bf16[8192,256]{1,0:T(8,128)(2,1)}) %all-gather.21.cloned.1.call-update) | async-done | bytes 4194320 | tf_op jit(solution)/shard_map/all_gather | solution.py:259
  338.3 6.7 gather_fusion.1
  360.3 6.8 convolution_convert_fusion.5
  367.2 28.5 %all-gather.31.cloned.1.call-done = bf16[1152,1024]{1,0:T(8,128)(2,1)} async-done(((bf16[1152,256]{1,0:T(8,128)(2,1)}), bf16[1152,1024]{1,0:T(8,128)(2,1)}) %all-gather.31.cloned.1.call-update) | async-done | bytes 2359312 | tf_op jit(solution)/shard_map/all_gather | solution.py:260
  403.3 6.2 fusion.13
  415.0 7.5 convolution_convert_fusion.1
  422.5 18.0 %reduce-scatter.18.cloned.1.call-done = bf16[1024,256]{1,0:T(8,128)(2,1)} async-done(((bf16[1024,1024]{1,0:T(8,128)(2,1)}), bf16[1024,256]{1,0:T(8,128)(2,1)}) %reduce-scatter.18.cloned.1.call-update) | async-done | bytes 524304 | tf_op jit(solution)/shard_map/reduce_scatter | solution.py:300
  440.7 48.8 %reduce-scatter.22.cloned.1.call-done = bf16[1152,256]{1,0:T(8,128)(2,1)} async-done(((bf16[1152,1024]{1,0:T(8,128)(2,1)}), bf16[1152,256]{1,0:T(8,128)(2,1)}) %reduce-scatter.22.cloned.1.call-update) | async-done | bytes 589840 | tf_op jit(solution)/shard_map/reduce_scatter | solution.py:300
  489.5 49.4 %reduce-scatter.20.cloned.1.call-done = bf16[1152,256]{1,0:T(8,128)(2,1)} async-done(((bf16[1152,1024]{1,0:T(8,128)(2,1)}), bf16[1152,256]{1,0:T(8,128)(2,1)}) %reduce-scatter.20.cloned.1.call-update) | async-done | bytes 589840 | tf_op jit(solution)/shard_map/reduce_scatter | solution.py:300
  538.9 13.5 %scatter_custom_fusion = bf16[8192,512]{1,0:T(8,128)(2,1)} fusion(s32[1152]{0:T(1024)S(1)} %get-tuple-element.97, bf16[]{:T(256)} %constant.74.clone.1, bf16[1152,256]{1,0:T(8,128)(2,1)} %reduce-scatter.22.cloned.1.call-done, bf16[]{:T(256)} %constant.86, bf16[1152,256]{1,0:T(8,128)(2,1)} %reduce-scatter.20.cloned.1.call-done), kind=kCustom, calls=%fused_computation.51 | custom fusion | flops 2359296 | bytes 9568260 | tf_op jit(solution)/shard_map/scatter | solution.py:350
  556.3 67.2 %reduce-scatter.24.cloned.1.call-done = bf16[1024,512]{1,0:T(8,128)(2,1)} async-done(((bf16[8192,512]{1,0:T(8,128)(2,1)}), bf16[1024,512]{1,0:T(8,128)(2,1)}) %reduce-scatter.24.cloned.1.call-update) | async-done | bytes 1048592 | tf_op jit(solution)/shard_map/reduce_scatter | solution.py:352
  626.4 43.1 %reduce-scatter.16.cloned.1.call-done = bf16[1024,256]{1,0:T(8,128)(2,1)} async-done(((bf16[1024,1024]{1,0:T(8,128)(2,1)}), bf16[1024,256]{1,0:T(8,128)(2,1)}) %reduce-scatter.16.cloned.1.call-update) | async-done | bytes 524304 | tf_op jit(solution)/shard_map/reduce_scatter | solution.py:300
  675.2 6.7 convolution_convert_fusion.2
  691.7 28.8 %all-gather.23.cloned.1.call-done = bf16[4,1032,256]{2,1,0:T(8,128)(2,1)} async-done(((bf16[1,1032,256]{2,1,0:T(8,128)(2,1)}), bf16[4,1032,256]{2,1,0:T(8,128)(2,1)}) %all-gather.23.cloned.1.call-update) | async-done | bytes 2113552 | tf_op jit(solution)/shard_map/all_gather | solution.py:362
  748.1 21.7 %reduce-scatter.28.cloned.1.call-done = bf16[128,1024]{1,0:T(8,128)(2,1)} async-done(((bf16[1024,1024]{1,0:T(8,128)(2,1)}), bf16[128,1024]{1,0:T(8,128)(2,1)}) %reduce-scatter.28.cloned.1.call-update) | async-done | bytes 262160
  771.7 42.9 %reduce-scatter.26.cloned.1.call-done = bf16[128,1024]{1,0:T(8,128)(2,1)} async-done(((bf16[1024,1024]{1,0:T(8,128)(2,1)}), bf16[128,1024]{1,0:T(8,128)(2,1)}) %reduce-scatter.26.cloned.1.call-update) | async-done | bytes 262160 | tf_op jit(solution)/shard_map/reduce_scatter | solution.py:386
  816.4 33.7 %flash_backward.1 = bf16[4,3,64,1024]{3,2,1,0:T(8,128)(2,1)} custom-call(bf16[4,3,64,1024]{3,2,1,0:T(8,128)(2,1)} %all-to-all-done.qkv_ref, bf16[4,64,1024]{2,1,0:T(8,128)(2,1)S(1)} %all-to-all-done.2.grad_ref, f32[4,64,1024]{2,1,0:T(8,128)S(1)} %get-tuple-element.42.wide_ref, f32[4,1,1024]{2,1,0:T(1,128)S(1)} %get-tuple-element.43.lse_ref), custom_call_target="tpu_custom_call" | custom-call | flops 32000000000 | bytes 8388608 | tf_op jit(solution)/shard_map/flash_backward/pallas_call | solution.py:180
  853.3 46.1 %all-gather.25.cloned.1.call-done = bf16[1024,1024]{1,0:T(8,128)(2,1)} async-done(((bf16[1024,256]{1,0:T(8,128)(2,1)}), bf16[1024,1024]{1,0:T(8,128)(2,1)}) %all-gather.25.cloned.1.call-update) | async-done | bytes 2097168 | tf_op jit(solution)/shard_map/all_gather | solution.py:356
  903.1 19.3 %all-to-all-done.3 = bf16[4,3,64,1024]{3,2,1,0:T(8,128)(2,1)S(1)} async-done(((bf16[4,3,64,1024]{3,2,1,0:T(8,128)(2,1)}), bf16[4,3,64,1024]{3,2,1,0:T(8,128)(2,1)S(1)}, u32[]{:S(2)}, u32[]{:S(2)}) %all-to-all-start.3) | async-done | bytes 1572896 | tf_op jit(solution)/shard_map/all_to_all | solution.py:394
  928.7 7.5 convolution_bitcast_fusion.1
  936.2 8.2 convolution_bitcast_fusion
  956.0 40.2 %psum.23 = f32[8,4,128]{2,1,0:T(4,128)S(1)} all-reduce(f32[8,4,128]{2,1,0:T(4,128)S(1)} %maximum_bitcast_fusion), channel_id=1, replica_groups=mesh['shard'=2,'ctx'=4,'tp'=4] {'shard','ctx','tp'}, use_global_device_ids=true, to_apply=%region_30.31 | all-reduce | flops 4096 | bytes 32768 | tf_op jit(solution)/shard_map/psum | solution.py:409
  997.3 16.2 %all-reduce.5.cloned.1.call-done = bf16[1024,1024]{1,0:T(8,128)(2,1)} async-done(((bf16[1024,1024]{1,0:T(8,128)(2,1)}), bf16[1024,1024]{1,0:T(8,128)(2,1)}) %all-reduce.5.cloned.1.call-update) | async-done | bytes 2097168 | tf_op jit(solution)/shard_map/psum | solution.py:400
  1021.0 33.4 %reduce-scatter.32.cloned.1.call-done = bf16[128,768]{1,0:T(8,128)(2,1)} async-done(((bf16[1024,768]{1,0:T(8,128)(2,1)}), bf16[128,768]{1,0:T(8,128)(2,1)}) %reduce-scatter.32.cloned.1.call-update) | async-done | bytes 196624
  (216 shorter events, 160.9 us)
Async XLA Ops:
  7.2 391.6 %copy-start = (bf16[1,1024,1024]{2,1,0:T(8,128)(2,1)S(1)}, bf16[1,1024,1024]{2,1,0:T(8,128)(2,1)}, u32[]{:S(2)}) copy-start(bf16[1,1024,1024]{2,1,0:T(8,128)(2,1)} %param.25) | copy-start | bytes 6291460
  7.2 37.6 %all-gather.15.cloned.1.call-start = ((), (), s32[]{:S(2)}) async-start(), calls=%async_computation.13 | async-start | bytes 1769472 | tf_op jit(solution)/shard_map/all_gather | solution.py:263
  9.1 78.3 %all-gather.27.cloned.1.call-start = ((), (), s32[]{:S(2)}) async-start(), calls=%async_computation.27 | async-start | bytes 4718592 | tf_op jit(solution)/shard_map/all_gather | solution.py:259
  11.1 149.1 %all-gather.17.cloned.1.call-start = ((), (), s32[]{:S(2)}) async-start(), calls=%async_computation.14 | async-start | bytes 2359296 | tf_op jit(solution)/shard_map/all_gather | solution.py:267
  11.8 148.3 %all-gather.19.cloned.1.call-start = ((), (), s32[]{:S(2)}) async-start(), calls=%async_computation.15 | async-start | bytes 2359296 | tf_op jit(solution)/shard_map/all_gather | solution.py:268
  50.1 44.1 %all-to-all-start = ((bf16[4,3,64,1024]{3,2,1,0:T(8,128)(2,1)}), bf16[4,3,64,1024]{3,2,1,0:T(8,128)(2,1)}, u32[]{:S(2)}, u32[]{:S(2)}) async-start(bf16[4,3,64,1024]{3,2,1,0:T(8,128)(2,1)} %bitcast.230), calls=%async_computation | async-start | bytes 3145728 | tf_op jit(solution)/shard_map/all_to_all | solution.py:278
  54.5 151.5 %all-gather.29.cloned.1.call-start = ((), (), s32[]{:S(2)}) async-start(), calls=%async_computation.28 | async-start | bytes 2949120 | tf_op jit(solution)/shard_map/all_gather | solution.py:260
  94.2 29.5 %copy-start.22 = (bf16[256,128]{1,0:T(8,128)(2,1)S(1)}, bf16[256,128]{1,0:T(8,128)(2,1)}, u32[]{:S(2)}) copy-start(bf16[256,128]{1,0:T(8,128)(2,1)} %param.20) | copy-start | bytes 196612
  119.5 37.4 %all-to-all-start.1 = ((bf16[4,64,1024]{2,1,0:T(8,128)(2,1)}), bf16[4,64,1024]{2,1,0:T(8,128)(2,1)}, u32[]{:S(2)}, u32[]{:S(2)}) async-start(bf16[4,64,1024]{2,1,0:T(8,128)(2,1)} %get-tuple-element.30), calls=%async_computation.1 | async-start | bytes 1048576 | tf_op jit(solution)/shard_map/all_to_all | solution.py:280
  123.6 169.5 %all-reduce.3.cloned.1.call-start = ((), (), s32[]{:S(2)}) async-start(), calls=%async_computation.16 | async-start | bytes 4194304 | tf_op jit(solution)/shard_map/psum | solution.py:289
  206.0 132.3 %all-gather.21.cloned.1.call-start = ((), (), s32[]{:S(2)}) async-start(), calls=%async_computation.17 | async-start | bytes 4718592 | tf_op jit(solution)/shard_map/all_gather | solution.py:259
  302.6 93.1 %all-gather.31.cloned.1.call-start = ((), (), s32[]{:S(2)}) async-start(), calls=%async_computation.29 | async-start | bytes 2949120 | tf_op jit(solution)/shard_map/all_gather | solution.py:260
  345.0 95.4 %reduce-scatter.18.cloned.1.call-start = ((), (), s32[]{:S(2)}) async-start(), calls=%async_computation.19 | async-start | bytes 2621440 | tf_op jit(solution)/shard_map/reduce_scatter | solution.py:300
  395.7 93.8 %reduce-scatter.22.cloned.1.call-start = ((), (), s32[]{:S(2)}) async-start(), calls=%async_computation.21 | async-start | bytes 2949120 | tf_op jit(solution)/shard_map/reduce_scatter | solution.py:300
  414.9 124.0 %reduce-scatter.20.cloned.1.call-start = ((), (), s32[]{:S(2)}) async-start(), calls=%async_computation.20 | async-start | bytes 2949120 | tf_op jit(solution)/shard_map/reduce_scatter | solution.py:300
  440.5 183.1 %reduce-scatter.24.cloned.1.call-start = ((), (), s32[]{:S(2)}) async-start(), calls=%async_computation.22 | async-start | bytes 9437184 | tf_op jit(solution)/shard_map/reduce_scatter | solution.py:352
  552.5 117.0 %reduce-scatter.16.cloned.1.call-start = ((), (), s32[]{:S(2)}) async-start(), calls=%async_computation.18 | async-start | bytes 2621440 | tf_op jit(solution)/shard_map/reduce_scatter | solution.py:300
  553.3 167.2 %all-gather.23.cloned.1.call-start = ((), (), s32[]{:S(2)}) async-start(), calls=%async_computation.23 | async-start | bytes 2641920 | tf_op jit(solution)/shard_map/all_gather | solution.py:362
  675.2 94.6 %reduce-scatter.28.cloned.1.call-start = ((), (), s32[]{:S(2)}) async-start(), calls=%async_computation.30 | async-start | bytes 2359296
  686.1 128.6 %reduce-scatter.26.cloned.1.call-start = ((), (), s32[]{:S(2)}) async-start(), calls=%async_computation.25 | async-start | bytes 2359296 | tf_op jit(solution)/shard_map/reduce_scatter | solution.py:386
  691.7 160.0 %reduce-scatter.30.cloned.1.call-start = ((), (), s32[]{:S(2)}) async-start(), calls=%async_computation.31 | async-start | bytes 589824
  743.9 72.5 %all-to-all-start.2 = ((bf16[4,64,1024]{2,1,0:T(8,128)(2,1)}), bf16[4,64,1024]{2,1,0:T(8,128)(2,1)S(1)}, u32[]{:S(2)}, u32[]{:S(2)}) async-start(bf16[4,64,1024]{2,1,0:T(8,128)(2,1)} %bitcast.28), calls=%async_computation.7 | async-start | bytes 1048576 | tf_op jit(solution)/shard_map/all_to_all | solution.py:382
  747.5 151.9 %all-gather.25.cloned.1.call-start = ((), (), s32[]{:S(2)}) async-start(), calls=%async_computation.24 | async-start | bytes 2621440 | tf_op jit(solution)/shard_map/all_gather | solution.py:356
  899.4 22.9 %all-to-all-start.3 = ((bf16[4,3,64,1024]{3,2,1,0:T(8,128)(2,1)}), bf16[4,3,64,1024]{3,2,1,0:T(8,128)(2,1)S(1)}, u32[]{:S(2)}, u32[]{:S(2)}) async-start(bf16[4,3,64,1024]{3,2,1,0:T(8,128)(2,1)} %flash_backward.1), calls=%async_computation.9 | async-start | bytes 3145728 | tf_op jit(solution)/shard_map/all_to_all | solution.py:394
  903.1 110.4 %all-reduce.5.cloned.1.call-start = ((), (), s32[]{:S(2)}) async-start(), calls=%async_computation.26 | async-start | bytes 4194304 | tf_op jit(solution)/shard_map/psum | solution.py:400
  928.3 126.1 %reduce-scatter.32.cloned.1.call-start = ((), (), s32[]{:S(2)}) async-start(), calls=%async_computation.32 | async-start | bytes 1769472
  936.2 9.2 copy-start.19
  936.2 9.2 copy-start.21
  936.2 9.2 copy-start.24
  936.2 9.2 copy-start.26
  936.2 9.2 copy-start.32
  1016.5 43.0 %copy-start.1 = (bf16[1,1024,1024]{2,1,0:T(8,128)(2,1)S(1)}, bf16[1,1024,1024]{2,1,0:T(8,128)(2,1)}, u32[]{:S(2)}) copy-start(bf16[1,1024,1024]{2,1,0:T(8,128)(2,1)} %param.25) | copy-start | bytes 6291460
  (29 other events, 114.7 us)
Sparse Core Ops, SparseCore 0:
  10.5 28.7 all-gather.14
  41.7 45.7 all-gather.26
  89.3 27.8 all-gather.16
  118.9 34.6 all-gather.18
  155.6 50.3 all-gather.28
  208.8 84.3 all-reduce.2
  302.7 35.6 all-gather.20
  345.1 50.5 all-gather.30
  398.6 41.8 reduce-scatter.17
  442.6 46.8 reduce-scatter.21
  491.8 47.0 reduce-scatter.19
  552.6 70.8 reduce-scatter.23
  625.8 43.6 reduce-scatter.15
  675.3 45.1 all-gather.22
  724.2 45.5 reduce-scatter.27
  773.5 41.1 reduce-scatter.25
  817.6 34.0 reduce-scatter.29
  853.1 46.2 all-gather.24
  928.4 85.0 all-reduce.4
  1016.6 37.7 reduce-scatter.31
